TPU v7x, 32 devices: a whole 2x2x4 slice. The times are simulated.
32 devices in a mesh: gx: 4 (over x, core), gy: 8 (over z, y).
Axes of the slice: x: 2, y: 2, z: 4, core: 2. Of those that a mesh axis runs over, the one named last changes fastest.
Arguments:
- east_velocity: float32 [48, 32, 2048], P(None, 'gx', 'gy'), may hold values from -3 to 3
- north_velocity: float32 [48, 32, 2048], P(None, 'gx', 'gy'), may hold values from -3 to 3
- salinity: float32 [48, 32, 2048], P(None, 'gx', 'gy'), may hold values from -6 to 6
- surface: float32 [32, 2048], P('gx', 'gy'), may hold values from -6 to 6
- column_depth: float32 [32, 2048], P('gx', 'gy'), may hold values from 0.5 to 4
- wet_column: int32 [32, 2048], P('gx', 'gy'), may hold values 0 or 1
- active_levels: int32 [32, 2048], P('gx', 'gy'), may hold values from 1 to 48
Outputs:
- east_flow: float32 [48, 32, 2048], P(None, 'gx', 'gy')
- north_flow: float32 [48, 32, 2048], P(None, 'gx', 'gy')
- salt_next: float32 [48, 32, 2048], P(None, 'gx', 'gy')
- surface_next: float32 [32, 2048], P('gx', 'gy')
All inputs are finite; a program needn't handle non-finite values. No bound on the sum of `wet_column` on one device may be relied on, other than what follows from the above.
Results may differ from a plain program's by a relative error of at most 0.000024.
Values sent between devices are 32-bit elements; how exact they have to be, the bound alone decides.
A program may use at most 64 MiB of HBM per device.

v0:
```python
import jax
import jax.numpy as jnp
from jax import lax
from jax.sharding import PartitionSpec as P

ITERS = 16


TIME_STEP = 0.2
CORIOLIS = 0.3
PRESS_COEF = 0.05
VISCOSITY = 0.1
DIFFUSIVITY = 0.1
SIGMA_SHIFT = 0.25
CHEB_CENTER = 3.625
CHEB_HALF = 3.375
DIVERGENCE_COEF = 8.0


def padded_2(cells, sides, width):
    for axis, dim in sides:
        count = lax.axis_size(axis)
        ends = count - 1
        head = lax.slice_in_dim(cells, 0, width, axis=dim)
        tail = lax.slice_in_dim(cells, cells.shape[dim] - width, cells.shape[dim], axis=dim)
        cells = jnp.concatenate(
            [
                lax.ppermute(tail, axis, [(i, (i + 1) % count) for i in range(ends)]),
                cells,
                lax.ppermute(head, axis, [((i + 1) % count, i) for i in range(ends)]),
            ],
            axis=dim,
        )
    return cells


def cheb_table(count):
    first = CHEB_CENTER / CHEB_HALF
    ratio = 1.0 / first
    keeps = []
    gains = []
    for index in range(count):
        ratio_next = 1.0 / (2.0 * first - ratio)
        keeps.append(ratio_next * ratio)
        gains.append(2.0 * ratio_next / CHEB_HALF)
        ratio = ratio_next
    return (keeps, gains)


def crop(array, width):
    if width == 0:
        return array
    return array[..., width : array.shape[-2] - width, width : array.shape[-1] - width]


def centre(field):
    return field[:, 2:-2, 2:-2]


def along_east(field):
    return (
        8.0 * (field[:, 3:-1, 2:-2] - field[:, 1:-3, 2:-2])
        - (field[:, 4:, 2:-2] - field[:, :-4, 2:-2])
    ) / 12.0


def along_north(field):
    return (
        8.0 * (field[:, 2:-2, 3:-1] - field[:, 2:-2, 1:-3])
        - (field[:, 2:-2, 4:] - field[:, 2:-2, :-4])
    ) / 12.0


def laplace(field):
    return (
        field[:, 3:-1, 2:-2]
        + field[:, 1:-3, 2:-2]
        + field[:, 2:-2, 3:-1]
        + field[:, 2:-2, 1:-3]
        - 4.0 * centre(field)
    )


def tendency(padded):
    east, north, tracer = (padded[0], padded[1], padded[2])
    pressure = PRESS_COEF * jnp.cumsum(tracer, axis=0)
    east_mid = centre(east)
    north_mid = centre(north)

    def advect(field):
        return -(east_mid * along_east(field) + north_mid * along_north(field))

    east_rate = (
        advect(east) + CORIOLIS * north_mid - along_east(pressure) + VISCOSITY * laplace(east)
    )
    north_rate = (
        advect(north) - CORIOLIS * east_mid - along_north(pressure) + VISCOSITY * laplace(north)
    )
    salt_rate = advect(tracer) + DIFFUSIVITY * laplace(tracer)
    return jnp.stack([east_rate, north_rate, salt_rate])


def nine_point(field, wet):
    weighted = wet * field
    edges = weighted[2:, 1:-1] + weighted[:-2, 1:-1] + weighted[1:-1, 2:] + weighted[1:-1, :-2]
    corners = weighted[2:, 2:] + weighted[2:, :-2] + weighted[:-2, 2:] + weighted[:-2, :-2]
    stencil = (20.0 * weighted[1:-1, 1:-1] - 4.0 * edges - corners) / 6.0
    wet_mid = wet[1:-1, 1:-1]
    field_mid = field[1:-1, 1:-1]
    return wet_mid * (SIGMA_SHIFT * field_mid + stencil) + (1.0 - wet_mid) * field_mid


def solver_rim(stacked, width):
    return padded_2(stacked, (("gx", 1), ("gy", 2)), width)


def chebyshev(right_side, start, wet):
    depth_rim = 4
    padded = solver_rim(jnp.stack([start, wet]), depth_rim)
    wet_pad = padded[1]
    residual = right_side - nine_point(crop(padded[0], depth_rim - 1), crop(wet_pad, depth_rim - 1))
    direction = residual / CHEB_CENTER
    keeps, gains = cheb_table(ITERS)
    keep_table = jnp.array(keeps, dtype=jnp.float32)
    gain_table = jnp.array(gains, dtype=jnp.float32)

    def sweep(outer, carry):
        solution, residual, direction = carry
        padded = solver_rim(jnp.stack([residual, direction]), depth_rim)
        res_pad, dir_pad = (padded[0], padded[1])
        for inner in range(depth_rim):
            solution = solution + crop(dir_pad, depth_rim - inner)
            image = nine_point(dir_pad, crop(wet_pad, inner))
            res_pad = crop(res_pad, 1) - image
            position = outer * depth_rim + inner
            dir_pad = keep_table[position] * crop(dir_pad, 1) + gain_table[position] * res_pad
        return (solution, res_pad, dir_pad)

    solution, residual, direction = lax.fori_loop(
        0, ITERS // depth_rim, sweep, (start, residual, direction)
    )
    return solution


def local(
    east_velocity, north_velocity, salinity, surface, column_depth, wet_column, active_levels
):
    wet = wet_column.astype(jnp.float32)
    levels = jnp.arange(east_velocity.shape[0], dtype=jnp.int32)
    mask3 = (levels[:, None, None] < active_levels[None]).astype(jnp.float32) * wet[None]

    def rate(state):
        padded = padded_2(state, (("gx", 2), ("gy", 3)), 2)
        return tendency(padded) * mask3

    state0 = jnp.stack([east_velocity, north_velocity, salinity]) * mask3
    state1 = state0 + TIME_STEP * rate(state0)
    state2 = 0.75 * state0 + 0.25 * (state1 + TIME_STEP * rate(state1))
    state3 = state0 / 3.0 + 2.0 / 3.0 * (state2 + TIME_STEP * rate(state2))
    level_count = east_velocity.shape[0]
    flow_east = column_depth * (jnp.sum(state3[0], axis=0) / level_count)
    flow_north = column_depth * (jnp.sum(state3[1], axis=0) / level_count)
    flows = padded_2(jnp.stack([flow_east, flow_north]), (("gx", 1), ("gy", 2)), 1)
    divergence = (flows[0, 2:, 1:-1] - flows[0, :-2, 1:-1]) * 0.5 + (
        flows[1, 1:-1, 2:] - flows[1, 1:-1, :-2]
    ) * 0.5
    right_side = wet * (SIGMA_SHIFT * surface - DIVERGENCE_COEF * divergence)
    solution = chebyshev(right_side, surface, wet)
    surface_pad = padded_2(solution, (("gx", 0), ("gy", 1)), 1)
    slope_east = (surface_pad[2:, 1:-1] - surface_pad[:-2, 1:-1]) * 0.5
    slope_north = (surface_pad[1:-1, 2:] - surface_pad[1:-1, :-2]) * 0.5
    east_flow = mask3 * (state3[0] - slope_east[None])
    north_flow = mask3 * (state3[1] - slope_north[None])
    return (east_flow, north_flow, state3[2], solution)


def solution(mesh):
    return jax.shard_map(
        local,
        mesh=mesh,
        in_specs=(
            P(None, "gx", "gy"),
            P(None, "gx", "gy"),
            P(None, "gx", "gy"),
            P("gx", "gy"),
            P("gx", "gy"),
            P("gx", "gy"),
            P("gx", "gy"),
        ),
        out_specs=(P(None, "gx", "gy"), P(None, "gx", "gy"), P(None, "gx", "gy"), P("gx", "gy")),
        check_vma=False,
    )
```

profile of v0, /device:TPU:22, one launch (start us, length us, event | category | flops | bytes accessed | tf_op | source)
XLA Modules:
  0.0 242.9 jit_solution(14355349683426717254)
XLA Ops:
  6.2 2.4 collective-permute-start.4
  10.5 3.8 %collective-permute-done.4 = f32[3,48,2,256]{3,2,1,0:T(2,128)S(1)} collective-permute-done((f32[3,48,2,256]{3,2,1,0:T(2,128)S(1)}, f32[3,48,2,256]{3,2,1,0:T(2,128)S(1)}, u32[]{:S(2)}, u32[]{:S(2)}) %collective-permute-start.4) | collective-permute-done | bytes 294944 | tf_op jit(solution)/shard_map/ppermute | solution.py:28
  17.9 2.4 collective-permute-start.7
  20.7 4.3 %collective-permute-start.6 = (f32[3,48,12,2]{1,3,2,0:T(2,128)S(1)}, f32[3,48,12,2]{1,3,2,0:T(2,128)S(1)}, u32[]{:S(2)}, u32[]{:S(2)}) collective-permute-start(f32[3,48,12,2]{1,3,2,0:T(2,128)S(1)} %copy.13), channel_id=1, source_target_pairs={{0,1},{1,2},{2,3},{3,4},{4,5},{5,6},{6,7},{8,9},{9,10},{10,11},{11... | collective-permute-start | bytes 41480 | tf_op jit(solution)/shard_map/ppermute | solution.py:28
  28.2 3.7 %pad_maximum_fusion.3 = f32[3,48,12,260]{3,2,1,0:T(8,128)S(1)} fusion(f32[3,48,12,2]{3,2,1,0:T(8,128)S(1)} %copy.16, f32[3,48,2,256]{3,2,1,0:T(2,128)S(1)} %collective-permute-done.5, f32[3,48,8,256]{3,2,1,0:T(8,128)S(1)} %maximum_multiply_fusion, f32[3,48,2,256]{3,2,1,0:T(2,128)S(1)} %collective-permute-done.4, f32[3,48,12,2]{3,2,1,0:T(8,128)} %copy.15), kind=kLoop, calls=%fused_computation.80 | loop fusion | flops 1797120 | bytes 3594240 | tf_op jit(solution)/shard_map/concatenate | solution.py:26
  38.6 2.4 collective-permute-start.8
  41.1 3.1 %collective-permute-start.21 = (f32[2,4,256]{2,1,0:T(4,128)S(1)}, f32[2,4,256]{2,1,0:T(4,128)S(1)}, u32[]{:S(2)}, u32[]{:S(2)}) collective-permute-start(f32[2,4,256]{2,1,0:T(4,128)S(1)} %get-tuple-element.282), channel_id=1, source_target_pairs={{8,0},{16,8},{24,16},{9,1},{17,9},{25,17},{10,2},{18,10},{26,18},{... | collective-permute-start | bytes 24584 | tf_op jit(solution)/shard_map/ppermute | solution.py:30
  50.9 4.3 %collective-permute-start.11 = (f32[3,48,12,2]{1,3,2,0:T(2,128)S(1)}, f32[3,48,12,2]{1,3,2,0:T(2,128)}, u32[]{:S(2)}, u32[]{:S(2)}) collective-permute-start(f32[3,48,12,2]{1,3,2,0:T(2,128)S(1)} %copy.18), channel_id=1, source_target_pairs={{1,0},{2,1},{3,2},{4,3},{5,4},{6,5},{7,6},{9,8},{10,9},{11,10},{12... | collective-permute-start | bytes 41480 | tf_op jit(solution)/shard_map/ppermute | solution.py:30
  55.2 2.3 copy.17
  57.5 2.9 %collective-permute-start.10 = (f32[3,48,12,2]{1,3,2,0:T(2,128)}, f32[3,48,12,2]{1,3,2,0:T(2,128)}, u32[]{:S(2)}, u32[]{:S(2)}) collective-permute-start(f32[3,48,12,2]{1,3,2,0:T(2,128)} %copy.17), channel_id=1, source_target_pairs={{0,1},{1,2},{2,3},{3,4},{4,5},{5,6},{6,7},{8,9},{9,10},{10,11},{11... | collective-permute-start | bytes 41480 | tf_op jit(solution)/shard_map/ppermute | solution.py:28
  60.5 2.3 copy.20
  63.6 2.3 copy.19
  65.9 4.1 %pad_maximum_fusion.4 = f32[3,48,12,260]{3,2,1,0:T(8,128)S(1)} fusion(f32[3,48,12,2]{3,2,1,0:T(8,128)} %copy.20, f32[3,48,2,256]{3,2,1,0:T(2,128)S(1)} %collective-permute-done.9, f32[3,48,8,256]{3,2,1,0:T(8,128)S(1)} %fusion.36, f32[3,48,2,256]{3,2,1,0:T(2,128)} %copy-done.14, f32[3,48,12,2]{3,2,1,0:T(8,128)} %copy.19), kind=kLoop, calls=%fused_computation.81 | loop fusion | flops 1797120 | bytes 3594240 | tf_op jit(solution)/shard_map/concatenate | solution.py:26
  76.2 2.0 collective-permute-start.13
  78.2 2.3 collective-permute-start.12
  81.2 2.8 %collective-permute-start.23 = (f32[2,16,4]{2,1,0:T(8,128)}, f32[2,16,4]{2,1,0:T(8,128)S(1)}, u32[]{:S(2)}, u32[]{:S(2)}) collective-permute-start(f32[2,16,4]{2,1,0:T(8,128)} %get-tuple-element.276), channel_id=1, source_target_pairs={{1,0},{2,1},{3,2},{4,3},{5,4},{6,5},{7,6},{9,8},{10,9},{11,10},{12... | collective-permute-start | bytes 1544 | tf_op jit(solution)/shard_map/ppermute | solution.py:30
  84.0 3.9 %collective-permute-start.22 = (f32[2,16,4]{2,1,0:T(8,128)S(1)}, f32[2,16,4]{2,1,0:T(8,128)}, u32[]{:S(2)}, u32[]{:S(2)}) collective-permute-start(f32[2,16,4]{2,1,0:T(8,128)S(1)} %get-tuple-element.275), channel_id=1, source_target_pairs={{0,1},{1,2},{2,3},{3,4},{4,5},{5,6},{6,7},{8,9},{9,10},{10,11},{11... | collective-permute-start | bytes 1544 | tf_op jit(solution)/shard_map/ppermute | solution.py:28
  93.8 2.3 copy.22
  96.1 3.8 %collective-permute-start.15 = (f32[3,48,12,2]{1,3,2,0:T(2,128)}, f32[3,48,12,2]{1,3,2,0:T(2,128)}, u32[]{:S(2)}, u32[]{:S(2)}) collective-permute-start(f32[3,48,12,2]{1,3,2,0:T(2,128)} %copy.22), channel_id=1, source_target_pairs={{1,0},{2,1},{3,2},{4,3},{5,4},{6,5},{7,6},{9,8},{10,9},{11,10},{12... | collective-permute-start | bytes 41480 | tf_op jit(solution)/shard_map/ppermute | solution.py:30
  99.9 2.3 copy.21
  102.1 3.1 %collective-permute-start.14 = (f32[3,48,12,2]{1,3,2,0:T(2,128)}, f32[3,48,12,2]{1,3,2,0:T(2,128)}, u32[]{:S(2)}, u32[]{:S(2)}) collective-permute-start(f32[3,48,12,2]{1,3,2,0:T(2,128)} %copy.21), channel_id=1, source_target_pairs={{0,1},{1,2},{2,3},{3,4},{4,5},{5,6},{6,7},{8,9},{9,10},{10,11},{11... | collective-permute-start | bytes 41480 | tf_op jit(solution)/shard_map/ppermute | solution.py:28
  105.3 2.3 copy.24
  108.3 2.3 copy.23
  110.6 4.1 %pad_maximum_fusion.5 = f32[3,48,12,260]{3,2,1,0:T(8,128)S(1)} fusion(f32[3,48,12,2]{3,2,1,0:T(8,128)} %copy.24, f32[3,48,2,256]{3,2,1,0:T(2,128)S(1)} %collective-permute-done.13, f32[3,48,8,256]{3,2,1,0:T(8,128)S(1)} %fusion.40, f32[3,48,2,256]{3,2,1,0:T(2,128)} %collective-permute-done.12, f32[3,48,12,2]{3,2,1,0:T(8,128)} %copy.23), kind=kLoop, calls=%fused_computation.82 | loop fusion | flops 1797120 | bytes 3594240 | tf_op jit(solution)/shard_map/concatenate | solution.py:26
  122.8 2.4 collective-permute-start.17
  125.3 2.4 collective-permute-done.17
  127.8 3.9 %collective-permute-start.19 = (f32[2,10,1]{2,1,0:T(8,128)S(1)}, f32[2,10,1]{2,1,0:T(8,128)S(1)}, u32[]{:S(2)}, u32[]{:S(2)}) collective-permute-start(f32[2,10,1]{2,1,0:T(8,128)S(1)} %get-tuple-element.274), channel_id=1, source_target_pairs={{0,1},{1,2},{2,3},{3,4},{4,5},{5,6},{6,7},{8,9},{9,10},{10,11},{11... | collective-permute-start | bytes 248 | tf_op jit(solution)/shard_map/ppermute | solution.py:28
  133.7 4.5 %collective-permute-done.18 = f32[2,10,1]{2,1,0:T(8,128)S(1)} collective-permute-done((f32[2,10,1]{2,1,0:T(8,128)S(1)}, f32[2,10,1]{2,1,0:T(8,128)S(1)}, u32[]{:S(2)}, u32[]{:S(2)}) %collective-permute-start.18) | collective-permute-done | bytes 112 | tf_op jit(solution)/shard_map/ppermute | solution.py:30
  138.4 85.9 %while.20 = (s32[]{:T(128)}, f32[8,256]{1,0:T(8,128)S(1)}, f32[8,256]{1,0:T(8,128)S(1)}, f32[8,256]{1,0:T(8,128)S(1)}, f32[16,264]{1,0:T(8,128)S(1)}, /*index=5*...) while((s32[]{:T(128)}, f32[8,256]{1,0:T(8,128)S(1)}, ...), condition=%wide.region_6.7_spmd.clone, body=%wide.region_5.6_spmd.sunk.clone.sunk | while | flops 332450 | bytes 1074181 | solution.py:139
  140.3 2.4 collective-permute-start.1
  142.8 2.5 %collective-permute-done.1 = f32[2,4,256]{2,1,0:T(4,128)S(1)} collective-permute-done((f32[2,4,256]{2,1,0:T(4,128)S(1)}, f32[2,4,256]{2,1,0:T(4,128)S(1)}, u32[]{:S(2)}, u32[]{:S(2)}) %collective-permute-start.1) | collective-permute-done | bytes 8224 | tf_op jit(solution)/shard_map/while/body/eval_jaxpr/ppermute | solution.py:28
  147.3 4.8 %collective-permute-start.3 = (f32[2,16,4]{2,1,0:T(8,128)S(1)}, f32[2,16,4]{2,1,0:T(8,128)S(1)}, u32[]{:S(2)}, u32[]{:S(2)}) collective-permute-start(f32[2,16,4]{2,1,0:T(8,128)S(1)} %get-tuple-element.354), channel_id=1, source_target_pairs={{0,1},{1,2},{2,3},{3,4},{4,5},{5,6},{6,7},{8,9},{9,10},{10,11},{11... | collective-permute-start | bytes 1544 | tf_op jit(solution)/shard_map/while/body/eval_jaxpr/ppermute | solution.py:28
  161.1 2.4 collective-permute-start.1
  163.6 2.5 %collective-permute-done.1 = f32[2,4,256]{2,1,0:T(4,128)S(1)} collective-permute-done((f32[2,4,256]{2,1,0:T(4,128)S(1)}, f32[2,4,256]{2,1,0:T(4,128)S(1)}, u32[]{:S(2)}, u32[]{:S(2)}) %collective-permute-start.1) | collective-permute-done | bytes 8224 | tf_op jit(solution)/shard_map/while/body/eval_jaxpr/ppermute | solution.py:28
  166.2 4.0 %collective-permute-start.2 = (f32[2,16,4]{2,1,0:T(8,128)S(1)}, f32[2,16,4]{2,1,0:T(8,128)S(1)}, u32[]{:S(2)}, u32[]{:S(2)}) collective-permute-start(f32[2,16,4]{2,1,0:T(8,128)S(1)} %get-tuple-element.353), channel_id=1, source_target_pairs={{1,0},{2,1},{3,2},{4,3},{5,4},{6,5},{7,6},{9,8},{10,9},{11,10},{12... | collective-permute-start | bytes 1544 | tf_op jit(solution)/shard_map/while/body/eval_jaxpr/ppermute | solution.py:30
  170.2 3.0 %collective-permute-start.3 = (f32[2,16,4]{2,1,0:T(8,128)S(1)}, f32[2,16,4]{2,1,0:T(8,128)S(1)}, u32[]{:S(2)}, u32[]{:S(2)}) collective-permute-start(f32[2,16,4]{2,1,0:T(8,128)S(1)} %get-tuple-element.354), channel_id=1, source_target_pairs={{0,1},{1,2},{2,3},{3,4},{4,5},{5,6},{6,7},{8,9},{9,10},{10,11},{11... | collective-permute-start | bytes 1544 | tf_op jit(solution)/shard_map/while/body/eval_jaxpr/ppermute | solution.py:28
  183.5 2.4 collective-permute-start.1
  185.9 2.5 %collective-permute-done.1 = f32[2,4,256]{2,1,0:T(4,128)S(1)} collective-permute-done((f32[2,4,256]{2,1,0:T(4,128)S(1)}, f32[2,4,256]{2,1,0:T(4,128)S(1)}, u32[]{:S(2)}, u32[]{:S(2)}) %collective-permute-start.1) | collective-permute-done | bytes 8224 | tf_op jit(solution)/shard_map/while/body/eval_jaxpr/ppermute | solution.py:28
  188.5 2.8 %collective-permute-start.2 = (f32[2,16,4]{2,1,0:T(8,128)S(1)}, f32[2,16,4]{2,1,0:T(8,128)S(1)}, u32[]{:S(2)}, u32[]{:S(2)}) collective-permute-start(f32[2,16,4]{2,1,0:T(8,128)S(1)} %get-tuple-element.353), channel_id=1, source_target_pairs={{1,0},{2,1},{3,2},{4,3},{5,4},{6,5},{7,6},{9,8},{10,9},{11,10},{12... | collective-permute-start | bytes 1544 | tf_op jit(solution)/shard_map/while/body/eval_jaxpr/ppermute | solution.py:30
  191.3 3.9 %collective-permute-start.3 = (f32[2,16,4]{2,1,0:T(8,128)S(1)}, f32[2,16,4]{2,1,0:T(8,128)S(1)}, u32[]{:S(2)}, u32[]{:S(2)}) collective-permute-start(f32[2,16,4]{2,1,0:T(8,128)S(1)} %get-tuple-element.354), channel_id=1, source_target_pairs={{0,1},{1,2},{2,3},{3,4},{4,5},{5,6},{6,7},{8,9},{9,10},{10,11},{11... | collective-permute-start | bytes 1544 | tf_op jit(solution)/shard_map/while/body/eval_jaxpr/ppermute | solution.py:28
  204.5 2.4 collective-permute-start.1
  207.0 2.5 %collective-permute-done.1 = f32[2,4,256]{2,1,0:T(4,128)S(1)} collective-permute-done((f32[2,4,256]{2,1,0:T(4,128)S(1)}, f32[2,4,256]{2,1,0:T(4,128)S(1)}, u32[]{:S(2)}, u32[]{:S(2)}) %collective-permute-start.1) | collective-permute-done | bytes 8224 | tf_op jit(solution)/shard_map/while/body/eval_jaxpr/ppermute | solution.py:28
  209.6 3.4 %collective-permute-start.2 = (f32[2,16,4]{2,1,0:T(8,128)S(1)}, f32[2,16,4]{2,1,0:T(8,128)S(1)}, u32[]{:S(2)}, u32[]{:S(2)}) collective-permute-start(f32[2,16,4]{2,1,0:T(8,128)S(1)} %get-tuple-element.353), channel_id=1, source_target_pairs={{1,0},{2,1},{3,2},{4,3},{5,4},{6,5},{7,6},{9,8},{10,9},{11,10},{12... | collective-permute-start | bytes 1544 | tf_op jit(solution)/shard_map/while/body/eval_jaxpr/ppermute | solution.py:30
  213.0 3.3 %collective-permute-start.3 = (f32[2,16,4]{2,1,0:T(8,128)S(1)}, f32[2,16,4]{2,1,0:T(8,128)S(1)}, u32[]{:S(2)}, u32[]{:S(2)}) collective-permute-start(f32[2,16,4]{2,1,0:T(8,128)S(1)} %get-tuple-element.354), channel_id=1, source_target_pairs={{0,1},{1,2},{2,3},{3,4},{4,5},{5,6},{6,7},{8,9},{9,10},{10,11},{11... | collective-permute-start | bytes 1544 | tf_op jit(solution)/shard_map/while/body/eval_jaxpr/ppermute | solution.py:28
  226.2 2.4 collective-permute-start.25
  228.6 2.5 %collective-permute-done.25 = f32[1,256]{1,0:T(1,128)S(1)} collective-permute-done((f32[1,256]{1,0:T(1,128)S(1)}, f32[1,256]{1,0:T(1,128)S(1)}, u32[]{:S(2)}, u32[]{:S(2)}) %collective-permute-start.25) | collective-permute-done | bytes 1056 | tf_op jit(solution)/shard_map/ppermute | solution.py:28
  231.2 4.2 %collective-permute-start.27 = (f32[10,1]{1,0:T(8,128)S(1)}, f32[10,1]{1,0:T(8,128)S(1)}, u32[]{:S(2)}, u32[]{:S(2)}) collective-permute-start(f32[10,1]{1,0:T(8,128)S(1)} %get-tuple-element.278), channel_id=1, source_target_pairs={{0,1},{1,2},{2,3},{3,4},{4,5},{5,6},{6,7},{8,9},{9,10},{10,11},{11... | collective-permute-start | bytes 128 | tf_op jit(solution)/shard_map/ppermute | solution.py:28
  237.4 4.5 %collective-permute-done.26 = f32[10,1]{1,0:T(8,128)S(1)} collective-permute-done((f32[10,1]{1,0:T(8,128)S(1)}, f32[10,1]{1,0:T(8,128)S(1)}, u32[]{:S(2)}, u32[]{:S(2)}) %collective-permute-start.26) | collective-permute-done | bytes 72 | tf_op jit(solution)/shard_map/ppermute | solution.py:30
  (180 shorter events, 97.4 us)
Async XLA Ops:
  4.3 6.1 %collective-permute-start.5 = (f32[3,48,2,256]{3,2,1,0:T(2,128)S(1)}, f32[3,48,2,256]{3,2,1,0:T(2,128)S(1)}, u32[]{:S(2)}, u32[]{:S(2)}) collective-permute-start(f32[3,48,2,256]{3,2,1,0:T(2,128)S(1)} %get-tuple-element.270), channel_id=1, source_target_pairs={{8,0},{16,8},{24,16},{9,1},{17,9},{25,17},{10,2},{18,10},{26,18},{... | collective-permute-start | bytes 884744 | tf_op jit(solution)/shard_map/ppermute | solution.py:30
  6.2 8.0 %collective-permute-start.4 = (f32[3,48,2,256]{3,2,1,0:T(2,128)S(1)}, f32[3,48,2,256]{3,2,1,0:T(2,128)S(1)}, u32[]{:S(2)}, u32[]{:S(2)}) collective-permute-start(f32[3,48,2,256]{3,2,1,0:T(2,128)S(1)} %get-tuple-element.269), channel_id=1, source_target_pairs={{0,8},{8,16},{16,24},{1,9},{9,17},{17,25},{2,10},{10,18},{18,26},{... | collective-permute-start | bytes 884744 | tf_op jit(solution)/shard_map/ppermute | solution.py:28
  17.9 7.2 %collective-permute-start.7 = (f32[3,48,12,2]{1,3,2,0:T(2,128)S(1)}, f32[3,48,12,2]{1,3,2,0:T(2,128)S(1)}, u32[]{:S(2)}, u32[]{:S(2)}) collective-permute-start(f32[3,48,12,2]{1,3,2,0:T(2,128)S(1)} %copy.14), channel_id=1, source_target_pairs={{1,0},{2,1},{3,2},{4,3},{5,4},{6,5},{7,6},{9,8},{10,9},{11,10},{12... | collective-permute-start | bytes 41480 | tf_op jit(solution)/shard_map/ppermute | solution.py:30
  20.7 5.9 %collective-permute-start.6 = (f32[3,48,12,2]{1,3,2,0:T(2,128)S(1)}, f32[3,48,12,2]{1,3,2,0:T(2,128)S(1)}, u32[]{:S(2)}, u32[]{:S(2)}) collective-permute-start(f32[3,48,12,2]{1,3,2,0:T(2,128)S(1)} %copy.13), channel_id=1, source_target_pairs={{0,1},{1,2},{2,3},{3,4},{4,5},{5,6},{6,7},{8,9},{9,10},{10,11},{11... | collective-permute-start | bytes 41480 | tf_op jit(solution)/shard_map/ppermute | solution.py:28
  36.7 9.5 %collective-permute-start.9 = (f32[3,48,2,256]{3,2,1,0:T(2,128)S(1)}, f32[3,48,2,256]{3,2,1,0:T(2,128)S(1)}, u32[]{:S(2)}, u32[]{:S(2)}) collective-permute-start(f32[3,48,2,256]{3,2,1,0:T(2,128)S(1)} %get-tuple-element.268), channel_id=1, source_target_pairs={{8,0},{16,8},{24,16},{9,1},{17,9},{25,17},{10,2},{18,10},{26,18},{... | collective-permute-start | bytes 884744 | tf_op jit(solution)/shard_map/ppermute | solution.py:30
  38.6 8.0 %collective-permute-start.8 = (f32[3,48,2,256]{3,2,1,0:T(2,128)S(1)}, f32[3,48,2,256]{3,2,1,0:T(2,128)S(1)}, u32[]{:S(2)}, u32[]{:S(2)}) collective-permute-start(f32[3,48,2,256]{3,2,1,0:T(2,128)S(1)} %get-tuple-element.267), channel_id=1, source_target_pairs={{0,8},{8,16},{16,24},{1,9},{9,17},{17,25},{2,10},{10,18},{18,26},{... | collective-permute-start | bytes 884744 | tf_op jit(solution)/shard_map/ppermute | solution.py:28
  41.1 19.3 %collective-permute-start.21 = (f32[2,4,256]{2,1,0:T(4,128)S(1)}, f32[2,4,256]{2,1,0:T(4,128)S(1)}, u32[]{:S(2)}, u32[]{:S(2)}) collective-permute-start(f32[2,4,256]{2,1,0:T(4,128)S(1)} %get-tuple-element.282), channel_id=1, source_target_pairs={{8,0},{16,8},{24,16},{9,1},{17,9},{25,17},{10,2},{18,10},{26,18},{... | collective-permute-start | bytes 24584 | tf_op jit(solution)/shard_map/ppermute | solution.py:30
  44.2 16.2 %collective-permute-start.20 = (f32[2,4,256]{2,1,0:T(4,128)S(1)}, f32[2,4,256]{2,1,0:T(4,128)S(1)}, u32[]{:S(2)}, u32[]{:S(2)}) collective-permute-start(f32[2,4,256]{2,1,0:T(4,128)S(1)} %get-tuple-element.281), channel_id=1, source_target_pairs={{0,8},{8,16},{16,24},{1,9},{9,17},{17,25},{2,10},{10,18},{18,26},{... | collective-permute-start | bytes 24584 | tf_op jit(solution)/shard_map/ppermute | solution.py:28
  50.9 9.5 %collective-permute-start.11 = (f32[3,48,12,2]{1,3,2,0:T(2,128)S(1)}, f32[3,48,12,2]{1,3,2,0:T(2,128)}, u32[]{:S(2)}, u32[]{:S(2)}) collective-permute-start(f32[3,48,12,2]{1,3,2,0:T(2,128)S(1)} %copy.18), channel_id=1, source_target_pairs={{1,0},{2,1},{3,2},{4,3},{5,4},{6,5},{7,6},{9,8},{10,9},{11,10},{12... | collective-permute-start | bytes 41480 | tf_op jit(solution)/shard_map/ppermute | solution.py:30
  57.5 6.2 %collective-permute-start.10 = (f32[3,48,12,2]{1,3,2,0:T(2,128)}, f32[3,48,12,2]{1,3,2,0:T(2,128)}, u32[]{:S(2)}, u32[]{:S(2)}) collective-permute-start(f32[3,48,12,2]{1,3,2,0:T(2,128)} %copy.17), channel_id=1, source_target_pairs={{0,1},{1,2},{2,3},{3,4},{4,5},{5,6},{6,7},{8,9},{9,10},{10,11},{11... | collective-permute-start | bytes 41480 | tf_op jit(solution)/shard_map/ppermute | solution.py:28
  71.8 2.5 %copy-start.7 = (f32[1,48,8,256]{3,2,1,0:T(8,128)}, f32[1,48,8,256]{3,2,1,0:T(8,128)S(1)}, u32[]{:S(2)}) copy-start(f32[1,48,8,256]{3,2,1,0:T(8,128)S(1)} %fusion.103) | copy-start | bytes 1179652
  76.2 14.3 %collective-permute-start.13 = (f32[3,48,2,256]{3,2,1,0:T(2,128)}, f32[3,48,2,256]{3,2,1,0:T(2,128)S(1)}, u32[]{:S(2)}, u32[]{:S(2)}) collective-permute-start(f32[3,48,2,256]{3,2,1,0:T(2,128)} %get-tuple-element.266), channel_id=1, source_target_pairs={{8,0},{16,8},{24,16},{9,1},{17,9},{25,17},{10,2},{18,10},{26,18},{... | collective-permute-start | bytes 884744 | tf_op jit(solution)/shard_map/ppermute | solution.py:30
  78.2 12.3 %collective-permute-start.12 = (f32[3,48,2,256]{3,2,1,0:T(2,128)}, f32[3,48,2,256]{3,2,1,0:T(2,128)}, u32[]{:S(2)}, u32[]{:S(2)}) collective-permute-start(f32[3,48,2,256]{3,2,1,0:T(2,128)} %get-tuple-element.265), channel_id=1, source_target_pairs={{0,8},{8,16},{16,24},{1,9},{9,17},{17,25},{2,10},{10,18},{18,26},{... | collective-permute-start | bytes 884744 | tf_op jit(solution)/shard_map/ppermute | solution.py:28
  81.2 6.8 %collective-permute-start.23 = (f32[2,16,4]{2,1,0:T(8,128)}, f32[2,16,4]{2,1,0:T(8,128)S(1)}, u32[]{:S(2)}, u32[]{:S(2)}) collective-permute-start(f32[2,16,4]{2,1,0:T(8,128)} %get-tuple-element.276), channel_id=1, source_target_pairs={{1,0},{2,1},{3,2},{4,3},{5,4},{6,5},{7,6},{9,8},{10,9},{11,10},{12... | collective-permute-start | bytes 1544 | tf_op jit(solution)/shard_map/ppermute | solution.py:30
  84.0 5.7 %collective-permute-start.22 = (f32[2,16,4]{2,1,0:T(8,128)S(1)}, f32[2,16,4]{2,1,0:T(8,128)}, u32[]{:S(2)}, u32[]{:S(2)}) collective-permute-start(f32[2,16,4]{2,1,0:T(8,128)S(1)} %get-tuple-element.275), channel_id=1, source_target_pairs={{0,1},{1,2},{2,3},{3,4},{4,5},{5,6},{6,7},{8,9},{9,10},{10,11},{11... | collective-permute-start | bytes 1544 | tf_op jit(solution)/shard_map/ppermute | solution.py:28
  96.1 9.2 %collective-permute-start.15 = (f32[3,48,12,2]{1,3,2,0:T(2,128)}, f32[3,48,12,2]{1,3,2,0:T(2,128)}, u32[]{:S(2)}, u32[]{:S(2)}) collective-permute-start(f32[3,48,12,2]{1,3,2,0:T(2,128)} %copy.22), channel_id=1, source_target_pairs={{1,0},{2,1},{3,2},{4,3},{5,4},{6,5},{7,6},{9,8},{10,9},{11,10},{12... | collective-permute-start | bytes 41480 | tf_op jit(solution)/shard_map/ppermute | solution.py:30
  102.1 6.2 %collective-permute-start.14 = (f32[3,48,12,2]{1,3,2,0:T(2,128)}, f32[3,48,12,2]{1,3,2,0:T(2,128)}, u32[]{:S(2)}, u32[]{:S(2)}) collective-permute-start(f32[3,48,12,2]{1,3,2,0:T(2,128)} %copy.21), channel_id=1, source_target_pairs={{0,1},{1,2},{2,3},{3,4},{4,5},{5,6},{6,7},{8,9},{9,10},{10,11},{11... | collective-permute-start | bytes 41480 | tf_op jit(solution)/shard_map/ppermute | solution.py:28
  117.9 1.3 copy-start.10
  117.9 1.4 copy-start.12
  120.1 18.2 %copy-start.18 = (s32[8,256]{1,0:T(8,128)S(1)}, s32[8,256]{1,0:T(8,128)}, u32[]{:S(2)}) copy-start(s32[8,256]{1,0:T(8,128)} %param.16) | copy-start | bytes 24580
  120.1 18.3 %copy-start.15 = (f32[16]{0:T(128)S(1)}, f32[16]{0:T(128)}, u32[]{:S(2)}) copy-start(f32[16]{0:T(128)} %constant.223.clone..sunk.2) | copy-start | bytes 196
  120.1 18.3 %copy-start.16 = (f32[16]{0:T(128)S(1)}, f32[16]{0:T(128)}, u32[]{:S(2)}) copy-start(f32[16]{0:T(128)} %constant.224.clone..sunk.2) | copy-start | bytes 196
  120.9 4.4 %collective-permute-start.16 = (f32[2,1,256]{2,1,0:T(1,128)S(1)}, f32[2,1,256]{2,1,0:T(1,128)S(1)}, u32[]{:S(2)}, u32[]{:S(2)}) collective-permute-start(f32[2,1,256]{2,1,0:T(1,128)S(1)} %get-tuple-element.280), channel_id=1, source_target_pairs={{8,0},{16,8},{24,16},{9,1},{17,9},{25,17},{10,2},{18,10},{26,18},{... | collective-permute-start | bytes 6152 | tf_op jit(solution)/shard_map/ppermute | solution.py:30
  122.8 4.9 %collective-permute-start.17 = (f32[2,1,256]{2,1,0:T(1,128)S(1)}, f32[2,1,256]{2,1,0:T(1,128)S(1)}, u32[]{:S(2)}, u32[]{:S(2)}) collective-permute-start(f32[2,1,256]{2,1,0:T(1,128)S(1)} %get-tuple-element.279), channel_id=1, source_target_pairs={{0,8},{8,16},{16,24},{1,9},{9,17},{17,25},{2,10},{10,18},{18,26},{... | collective-permute-start | bytes 6152 | tf_op jit(solution)/shard_map/ppermute | solution.py:28
  127.8 5.9 %collective-permute-start.19 = (f32[2,10,1]{2,1,0:T(8,128)S(1)}, f32[2,10,1]{2,1,0:T(8,128)S(1)}, u32[]{:S(2)}, u32[]{:S(2)}) collective-permute-start(f32[2,10,1]{2,1,0:T(8,128)S(1)} %get-tuple-element.274), channel_id=1, source_target_pairs={{0,1},{1,2},{2,3},{3,4},{4,5},{5,6},{6,7},{8,9},{9,10},{10,11},{11... | collective-permute-start | bytes 248 | tf_op jit(solution)/shard_map/ppermute | solution.py:28
  131.7 6.5 %collective-permute-start.18 = (f32[2,10,1]{2,1,0:T(8,128)S(1)}, f32[2,10,1]{2,1,0:T(8,128)S(1)}, u32[]{:S(2)}, u32[]{:S(2)}) collective-permute-start(f32[2,10,1]{2,1,0:T(8,128)S(1)} %get-tuple-element.273), channel_id=1, source_target_pairs={{1,0},{2,1},{3,2},{4,3},{5,4},{6,5},{7,6},{9,8},{10,9},{11,10},{12... | collective-permute-start | bytes 248 | tf_op jit(solution)/shard_map/ppermute | solution.py:30
  138.4 103.6 %copy-start.17 = (s32[8,256]{1,0:T(8,128)S(1)}, s32[8,256]{1,0:T(8,128)}, u32[]{:S(2)}) copy-start(s32[8,256]{1,0:T(8,128)} %param.17) | copy-start | bytes 24580
  138.4 4.4 %collective-permute-start = (f32[2,4,256]{2,1,0:T(4,128)S(1)}, f32[2,4,256]{2,1,0:T(4,128)S(1)}, u32[]{:S(2)}, u32[]{:S(2)}) collective-permute-start(f32[2,4,256]{2,1,0:T(4,128)S(1)} %get-tuple-element.351), channel_id=1, source_target_pairs={{8,0},{16,8},{24,16},{9,1},{17,9},{25,17},{10,2},{18,10},{26,18},{... | collective-permute-start | bytes 24584 | tf_op jit(solution)/shard_map/while/body/eval_jaxpr/ppermute | solution.py:30
  140.3 5.0 %collective-permute-start.1 = (f32[2,4,256]{2,1,0:T(4,128)S(1)}, f32[2,4,256]{2,1,0:T(4,128)S(1)}, u32[]{:S(2)}, u32[]{:S(2)}) collective-permute-start(f32[2,4,256]{2,1,0:T(4,128)S(1)} %get-tuple-element.352), channel_id=1, source_target_pairs={{0,8},{8,16},{16,24},{1,9},{9,17},{17,25},{2,10},{10,18},{18,26},{... | collective-permute-start | bytes 24584 | tf_op jit(solution)/shard_map/while/body/eval_jaxpr/ppermute | solution.py:28
  145.4 7.4 %collective-permute-start.2 = (f32[2,16,4]{2,1,0:T(8,128)S(1)}, f32[2,16,4]{2,1,0:T(8,128)S(1)}, u32[]{:S(2)}, u32[]{:S(2)}) collective-permute-start(f32[2,16,4]{2,1,0:T(8,128)S(1)} %get-tuple-element.353), channel_id=1, source_target_pairs={{1,0},{2,1},{3,2},{4,3},{5,4},{6,5},{7,6},{9,8},{10,9},{11,10},{12... | collective-permute-start | bytes 1544 | tf_op jit(solution)/shard_map/while/body/eval_jaxpr/ppermute | solution.py:30
  147.3 6.3 %collective-permute-start.3 = (f32[2,16,4]{2,1,0:T(8,128)S(1)}, f32[2,16,4]{2,1,0:T(8,128)S(1)}, u32[]{:S(2)}, u32[]{:S(2)}) collective-permute-start(f32[2,16,4]{2,1,0:T(8,128)S(1)} %get-tuple-element.354), channel_id=1, source_target_pairs={{0,1},{1,2},{2,3},{3,4},{4,5},{5,6},{6,7},{8,9},{9,10},{10,11},{11... | collective-permute-start | bytes 1544 | tf_op jit(solution)/shard_map/while/body/eval_jaxpr/ppermute | solution.py:28
  159.2 4.4 %collective-permute-start = (f32[2,4,256]{2,1,0:T(4,128)S(1)}, f32[2,4,256]{2,1,0:T(4,128)S(1)}, u32[]{:S(2)}, u32[]{:S(2)}) collective-permute-start(f32[2,4,256]{2,1,0:T(4,128)S(1)} %get-tuple-element.351), channel_id=1, source_target_pairs={{8,0},{16,8},{24,16},{9,1},{17,9},{25,17},{10,2},{18,10},{26,18},{... | collective-permute-start | bytes 24584 | tf_op jit(solution)/shard_map/while/body/eval_jaxpr/ppermute | solution.py:30
  161.1 5.0 %collective-permute-start.1 = (f32[2,4,256]{2,1,0:T(4,128)S(1)}, f32[2,4,256]{2,1,0:T(4,128)S(1)}, u32[]{:S(2)}, u32[]{:S(2)}) collective-permute-start(f32[2,4,256]{2,1,0:T(4,128)S(1)} %get-tuple-element.352), channel_id=1, source_target_pairs={{0,8},{8,16},{16,24},{1,9},{9,17},{17,25},{2,10},{10,18},{18,26},{... | collective-permute-start | bytes 24584 | tf_op jit(solution)/shard_map/while/body/eval_jaxpr/ppermute | solution.py:28
  166.2 7.7 %collective-permute-start.2 = (f32[2,16,4]{2,1,0:T(8,128)S(1)}, f32[2,16,4]{2,1,0:T(8,128)S(1)}, u32[]{:S(2)}, u32[]{:S(2)}) collective-permute-start(f32[2,16,4]{2,1,0:T(8,128)S(1)} %get-tuple-element.353), channel_id=1, source_target_pairs={{1,0},{2,1},{3,2},{4,3},{5,4},{6,5},{7,6},{9,8},{10,9},{11,10},{12... | collective-permute-start | bytes 1544 | tf_op jit(solution)/shard_map/while/body/eval_jaxpr/ppermute | solution.py:30
  170.2 5.6 %collective-permute-start.3 = (f32[2,16,4]{2,1,0:T(8,128)S(1)}, f32[2,16,4]{2,1,0:T(8,128)S(1)}, u32[]{:S(2)}, u32[]{:S(2)}) collective-permute-start(f32[2,16,4]{2,1,0:T(8,128)S(1)} %get-tuple-element.354), channel_id=1, source_target_pairs={{0,1},{1,2},{2,3},{3,4},{4,5},{5,6},{6,7},{8,9},{9,10},{10,11},{11... | collective-permute-start | bytes 1544 | tf_op jit(solution)/shard_map/while/body/eval_jaxpr/ppermute | solution.py:28
  181.5 4.4 %collective-permute-start = (f32[2,4,256]{2,1,0:T(4,128)S(1)}, f32[2,4,256]{2,1,0:T(4,128)S(1)}, u32[]{:S(2)}, u32[]{:S(2)}) collective-permute-start(f32[2,4,256]{2,1,0:T(4,128)S(1)} %get-tuple-element.351), channel_id=1, source_target_pairs={{8,0},{16,8},{24,16},{9,1},{17,9},{25,17},{10,2},{18,10},{26,18},{... | collective-permute-start | bytes 24584 | tf_op jit(solution)/shard_map/while/body/eval_jaxpr/ppermute | solution.py:30
  183.5 5.0 %collective-permute-start.1 = (f32[2,4,256]{2,1,0:T(4,128)S(1)}, f32[2,4,256]{2,1,0:T(4,128)S(1)}, u32[]{:S(2)}, u32[]{:S(2)}) collective-permute-start(f32[2,4,256]{2,1,0:T(4,128)S(1)} %get-tuple-element.352), channel_id=1, source_target_pairs={{0,8},{8,16},{16,24},{1,9},{9,17},{17,25},{2,10},{10,18},{18,26},{... | collective-permute-start | bytes 24584 | tf_op jit(solution)/shard_map/while/body/eval_jaxpr/ppermute | solution.py:28
  188.5 7.4 %collective-permute-start.2 = (f32[2,16,4]{2,1,0:T(8,128)S(1)}, f32[2,16,4]{2,1,0:T(8,128)S(1)}, u32[]{:S(2)}, u32[]{:S(2)}) collective-permute-start(f32[2,16,4]{2,1,0:T(8,128)S(1)} %get-tuple-element.353), channel_id=1, source_target_pairs={{1,0},{2,1},{3,2},{4,3},{5,4},{6,5},{7,6},{9,8},{10,9},{11,10},{12... | collective-permute-start | bytes 1544 | tf_op jit(solution)/shard_map/while/body/eval_jaxpr/ppermute | solution.py:30
  191.3 5.6 %collective-permute-start.3 = (f32[2,16,4]{2,1,0:T(8,128)S(1)}, f32[2,16,4]{2,1,0:T(8,128)S(1)}, u32[]{:S(2)}, u32[]{:S(2)}) collective-permute-start(f32[2,16,4]{2,1,0:T(8,128)S(1)} %get-tuple-element.354), channel_id=1, source_target_pairs={{0,1},{1,2},{2,3},{3,4},{4,5},{5,6},{6,7},{8,9},{9,10},{10,11},{11... | collective-permute-start | bytes 1544 | tf_op jit(solution)/shard_map/while/body/eval_jaxpr/ppermute | solution.py:28
  202.6 4.4 %collective-permute-start = (f32[2,4,256]{2,1,0:T(4,128)S(1)}, f32[2,4,256]{2,1,0:T(4,128)S(1)}, u32[]{:S(2)}, u32[]{:S(2)}) collective-permute-start(f32[2,4,256]{2,1,0:T(4,128)S(1)} %get-tuple-element.351), channel_id=1, source_target_pairs={{8,0},{16,8},{24,16},{9,1},{17,9},{25,17},{10,2},{18,10},{26,18},{... | collective-permute-start | bytes 24584 | tf_op jit(solution)/shard_map/while/body/eval_jaxpr/ppermute | solution.py:30
  204.5 5.0 %collective-permute-start.1 = (f32[2,4,256]{2,1,0:T(4,128)S(1)}, f32[2,4,256]{2,1,0:T(4,128)S(1)}, u32[]{:S(2)}, u32[]{:S(2)}) collective-permute-start(f32[2,4,256]{2,1,0:T(4,128)S(1)} %get-tuple-element.352), channel_id=1, source_target_pairs={{0,8},{8,16},{16,24},{1,9},{9,17},{17,25},{2,10},{10,18},{18,26},{... | collective-permute-start | bytes 24584 | tf_op jit(solution)/shard_map/while/body/eval_jaxpr/ppermute | solution.py:28
  209.6 7.4 %collective-permute-start.2 = (f32[2,16,4]{2,1,0:T(8,128)S(1)}, f32[2,16,4]{2,1,0:T(8,128)S(1)}, u32[]{:S(2)}, u32[]{:S(2)}) collective-permute-start(f32[2,16,4]{2,1,0:T(8,128)S(1)} %get-tuple-element.353), channel_id=1, source_target_pairs={{1,0},{2,1},{3,2},{4,3},{5,4},{6,5},{7,6},{9,8},{10,9},{11,10},{12... | collective-permute-start | bytes 1544 | tf_op jit(solution)/shard_map/while/body/eval_jaxpr/ppermute | solution.py:30
  213.0 5.6 %collective-permute-start.3 = (f32[2,16,4]{2,1,0:T(8,128)S(1)}, f32[2,16,4]{2,1,0:T(8,128)S(1)}, u32[]{:S(2)}, u32[]{:S(2)}) collective-permute-start(f32[2,16,4]{2,1,0:T(8,128)S(1)} %get-tuple-element.354), channel_id=1, source_target_pairs={{0,1},{1,2},{2,3},{3,4},{4,5},{5,6},{6,7},{8,9},{9,10},{10,11},{11... | collective-permute-start | bytes 1544 | tf_op jit(solution)/shard_map/while/body/eval_jaxpr/ppermute | solution.py:28
  224.3 18.7 %copy-start.13 = (f32[8,256]{1,0:T(8,128)}, f32[8,256]{1,0:T(8,128)S(1)}, u32[]{:S(2)}) copy-start(f32[8,256]{1,0:T(8,128)S(1)} %get-tuple-element.181) | copy-start | bytes 24580
  224.3 4.3 %collective-permute-start.24 = (f32[1,256]{1,0:T(1,128)S(1)}, f32[1,256]{1,0:T(1,128)S(1)}, u32[]{:S(2)}, u32[]{:S(2)}) collective-permute-start(f32[1,256]{1,0:T(1,128)S(1)} %get-tuple-element.285), channel_id=1, source_target_pairs={{8,0},{16,8},{24,16},{9,1},{17,9},{25,17},{10,2},{18,10},{26,18},{... | collective-permute-start | bytes 3080 | tf_op jit(solution)/shard_map/ppermute | solution.py:30
  226.2 4.9 %collective-permute-start.25 = (f32[1,256]{1,0:T(1,128)S(1)}, f32[1,256]{1,0:T(1,128)S(1)}, u32[]{:S(2)}, u32[]{:S(2)}) collective-permute-start(f32[1,256]{1,0:T(1,128)S(1)} %get-tuple-element.286), channel_id=1, source_target_pairs={{0,8},{8,16},{16,24},{1,9},{9,17},{17,25},{2,10},{10,18},{18,26},{... | collective-permute-start | bytes 3080 | tf_op jit(solution)/shard_map/ppermute | solution.py:28
  231.2 6.2 %collective-permute-start.27 = (f32[10,1]{1,0:T(8,128)S(1)}, f32[10,1]{1,0:T(8,128)S(1)}, u32[]{:S(2)}, u32[]{:S(2)}) collective-permute-start(f32[10,1]{1,0:T(8,128)S(1)} %get-tuple-element.278), channel_id=1, source_target_pairs={{0,1},{1,2},{2,3},{3,4},{4,5},{5,6},{6,7},{8,9},{9,10},{10,11},{11... | collective-permute-start | bytes 128 | tf_op jit(solution)/shard_map/ppermute | solution.py:28
  235.4 6.4 %collective-permute-start.26 = (f32[10,1]{1,0:T(8,128)S(1)}, f32[10,1]{1,0:T(8,128)S(1)}, u32[]{:S(2)}, u32[]{:S(2)}) collective-permute-start(f32[10,1]{1,0:T(8,128)S(1)} %get-tuple-element.277), channel_id=1, source_target_pairs={{1,0},{2,1},{3,2},{4,3},{5,4},{6,5},{7,6},{9,8},{10,9},{11,10},{12... | collective-permute-start | bytes 128 | tf_op jit(solution)/shard_map/ppermute | solution.py:30
  (12 other events, 12.8 us)
where the time goes:
time: 245 us; the launch traced here: 243 us
  starting transfers between devices  111 us (45%)
  other arithmetic  55.5 us (23%)
  waiting for transfers between devices  39.8 us (16%)
  local copies, waits for them, and re-layouts  34.9 us (14%)
    ppermute x20, starting transfers between devices, padded_2(): lax.ppermute(tail, axis, [(i, (i + 1) % count) for i in range(ends)])  60.9 us
    ppermute x20, starting transfers between devices, padded_2(): lax.ppermute(head, axis, [((i + 1) % count, i) for i in range(ends)])  49.9 us
    ppermute x20, waiting for transfers between devices, padded_2(): lax.ppermute(tail, axis, [(i, (i + 1) % count) for i in range(ends)])  28.9 us
    mul x17, other arithmetic, nine_point(): weighted = wet * field  16.5 us
    concatenate x18, other arithmetic, padded_2(): jnp.concatenate([lax.ppermute(tail, axis, [(i, (i + 1) % count) for i in...  15.5 us
    slice x14, local copies, waits for them, and re-layouts, padded_2(): lax.slice_in_dim(cells, cells.shape[dim] - width, cells.shape[dim], axis=...  12.4 us
    another operation x9, other arithmetic, tendency(): return jnp.stack([east_rate, north_rate, salt_rate])  11.3 us
    ppermute x20, waiting for transfers between devices, padded_2(): lax.ppermute(head, axis, [((i + 1) % count, i) for i in range(ends)])  10.9 us
  transfers between devices with their start and end apart: 40, of which 19 were waited for; matrix products, arithmetic and copies ran while one was open for 8% of the time, Pallas kernels for 0%

commit v1 on v0

v1 whole, which is shorter than its diff:
```python
import functools

import jax
import jax.numpy as jnp
from jax import lax
from jax.experimental import pallas as pl
from jax.experimental.pallas import tpu as pltpu
from jax.sharding import PartitionSpec as P

ITERS = 16

TIME_STEP = 0.2
CORIOLIS = 0.3
PRESS_COEF = 0.05
VISCOSITY = 0.1
DIFFUSIVITY = 0.1
SIGMA_SHIFT = 0.25
CHEB_CENTER = 3.625
CHEB_HALF = 3.375
DIVERGENCE_COEF = 8.0

ROWS = 8
LANES = 128
CHUNK = 8
MESH = pl.DeviceIdType.MESH


def cheb_table(count):
    first = CHEB_CENTER / CHEB_HALF
    ratio = 1.0 / first
    keeps = []
    gains = []
    for index in range(count):
        ratio_next = 1.0 / (2.0 * first - ratio)
        keeps.append(ratio_next * ratio)
        gains.append(2.0 * ratio_next / CHEB_HALF)
        ratio = ratio_next
    return (keeps, gains)


def kernel(
    nx, ny, reach, slots,
    east_ref, north_ref, salt_ref, surface_ref, depth_ref, wet_ref, active_ref,
    east_out, north_out, salt_out, surface_out,
    q0, qa, qb, send_x, recv_x, send_y, recv_y,
    stat_c, stat_e, flow_c, flow_e, all_stat, rim_stat, all_flow, rim_flow, xs,
    x_send, x_recv, y_send, y_recv,
    stat_send, stat_recv, stat_rim_send, stat_rim_recv,
    flow_send, flow_recv, flow_rim_send, flow_rim_recv,
):
    gx = lax.axis_index("gx")
    gy = lax.axis_index("gy")
    levels = east_ref.shape[0]
    width = east_ref.shape[2]
    tiles = width // LANES
    chunks = levels // CHUNK
    groups = 3 * CHUNK // 4
    relative = slots < nx
    row = lax.broadcasted_iota(jnp.int32, (ROWS, LANES), 0)
    lane = lax.broadcasted_iota(jnp.int32, (ROWS, LANES), 1)
    pair = row // 2
    zero = jnp.zeros((ROWS, LANES), jnp.float32)

    def lanes(t):
        return slice(t * LANES, (t + 1) * LANES)

    def slot_in(owner, peer):
        return owner - peer + reach if relative else owner

    def inside(x, y):
        return jnp.logical_and(
            jnp.logical_and(x >= 0, x < nx), jnp.logical_and(y >= 0, y < ny)
        )

    offsets = [o for o in range(-reach, reach + 1)]
    partners = [(o, side) for o in offsets for side in (-1, 0, 1) if (o, side) != (0, 0)]

    barrier = pltpu.get_barrier_semaphore()
    count = jnp.int32(0)
    for o, side in partners:
        there = inside(gx + o, gy + side)

        @pl.when(there)
        def _(o=o, side=side):
            pl.semaphore_signal(
                barrier, inc=1, device_id=(gx + o, gy + side), device_id_type=MESH
            )

        count = count + there.astype(jnp.int32)

    own = slot_in(gx, gx)

    for side, missing in ((0, gx == 0), (1, gx == nx - 1)):
        @pl.when(missing)
        def _(side=side):
            for stage in range(3):
                @pl.loop(0, chunks)
                def _(c, stage=stage):
                    recv_x[stage, side, c] = jnp.zeros((groups, ROWS, width), jnp.float32)

    for side, missing in ((0, gy == 0), (1, gy == ny - 1)):
        @pl.when(missing)
        def _(side=side):
            recv_y[:, side] = jnp.zeros((3, chunks, ROWS, LANES), jnp.float32)
            rim_stat[side] = jnp.zeros((slots, 2, ROWS, LANES), jnp.float32)
            rim_flow[side] = jnp.zeros((slots, 2, ROWS, LANES), jnp.float32)

    if relative:
        for o in offsets:
            @pl.when(jnp.logical_not(inside(gx + o, gy)))
            def _(o=o):
                for block in (all_stat, all_flow):
                    block[o + reach] = jnp.zeros((2, ROWS, width), jnp.float32)
                for block in (rim_stat, rim_flow):
                    for side in range(2):
                        block[side, o + reach] = jnp.zeros((2, ROWS, LANES), jnp.float32)

    def pack(state, stage, c):
        rim = zero
        for f in range(3):
            for half in range(CHUNK // 4):
                group = f * (CHUNK // 4) + half
                ups = [None] * tiles
                downs = [None] * tiles
                for m in range(4):
                    k = c * CHUNK + half * 4 + m
                    position = group * 4 + m
                    parts = [state[f, k, :, lanes(t)] for t in range(tiles)]
                    for t in range(tiles):
                        turned = parts[t] if m == 3 else pltpu.roll(parts[t], 2 * m + 2, 0)
                        if m == 0:
                            ups[t] = turned
                            downs[t] = turned
                        else:
                            ups[t] = jnp.where(pair == m, turned, ups[t])
                            downs[t] = jnp.where(pair == (m + 1) % 4, turned, downs[t])
                    ends = jnp.where(lane < LANES // 2, parts[0], parts[-1])
                    rim = jnp.where(
                        lane // 4 == position,
                        pltpu.roll(ends, (4 * position + 2) % LANES, 1),
                        rim,
                    )
                for t in range(tiles):
                    send_x[stage, 0, c, group, :, lanes(t)] = downs[t]
                    send_x[stage, 1, c, group, :, lanes(t)] = ups[t]
        send_y[stage, c] = rim

    def x_copy(stage, c, side):
        return pltpu.make_async_remote_copy(
            src_ref=send_x.at[stage, side, c],
            dst_ref=recv_x.at[stage, 1 - side, c],
            send_sem=x_send.at[stage, side, c],
            recv_sem=x_recv.at[stage, 1 - side, c],
            device_id=(gx + 2 * side - 1, gy),
            device_id_type=MESH,
        )

    def y_copy(stage, c, side):
        return pltpu.make_async_remote_copy(
            src_ref=send_y.at[stage, c],
            dst_ref=recv_y.at[stage, 1 - side, c],
            send_sem=y_send.at[stage, side, c],
            recv_sem=y_recv.at[stage, 1 - side, c],
            device_id=(gx, gy + 2 * side - 1),
            device_id_type=MESH,
        )

    near = [
        (x_copy, 0, gx > 0), (x_copy, 1, gx < nx - 1),
        (y_copy, 0, gy > 0), (y_copy, 1, gy < ny - 1),
    ]

    def launch(stage, c):
        for copy, side, there in near:
            @pl.when(there)
            def _(copy=copy, side=side):
                copy(stage, c, side).start()

    def arrive(stage, c):
        for copy, side, there in near:
            @pl.when(there)
            def _(copy=copy, side=side):
                copy(stage, c, 1 - side).wait_recv()

    def drain(stage, c):
        for copy, side, there in near:
            @pl.when(there)
            def _(copy=copy, side=side):
                copy(stage, c, side).wait_send()

    def far_copy(kind, o, side):
        block, rim, everything, edge, ss, rs, rss, rrs = kind
        slot = slot_in(gx, gx + o)
        if side == 0:
            return pltpu.make_async_remote_copy(
                src_ref=block, dst_ref=everything.at[slot],
                send_sem=ss.at[o + reach], recv_sem=rs.at[slot],
                device_id=(gx + o, gy), device_id_type=MESH,
            )
        to = (1 - side) // 2
        return pltpu.make_async_remote_copy(
            src_ref=rim, dst_ref=edge.at[to, slot],
            send_sem=rss.at[to, o + reach], recv_sem=rrs.at[to, slot],
            device_id=(gx + o, gy + side), device_id_type=MESH,
        )

    def far_wait(kind, o, side):
        block, rim, everything, edge, ss, rs, rss, rrs = kind
        slot = slot_in(gx + o, gx)
        if side == 0:
            pltpu.make_async_remote_copy(
                src_ref=block, dst_ref=everything.at[slot],
                send_sem=ss.at[o + reach], recv_sem=rs.at[slot],
                device_id=(gx + o, gy), device_id_type=MESH,
            ).wait_recv()
        else:
            at = (1 + side) // 2
            pltpu.make_async_remote_copy(
                src_ref=rim, dst_ref=edge.at[at, slot],
                send_sem=rss.at[at, o + reach], recv_sem=rrs.at[at, slot],
                device_id=(gx + o, gy + side), device_id_type=MESH,
            ).wait_recv()

    def far(action):
        for o, side in partners:
            @pl.when(inside(gx + o, gy + side))
            def _(o=o, side=side):
                action(o, side)

    stat_kind = (stat_c, stat_e, all_stat, rim_stat,
                 stat_send, stat_recv, stat_rim_send, stat_rim_recv)
    flow_kind = (flow_c, flow_e, all_flow, rim_flow,
                 flow_send, flow_recv, flow_rim_send, flow_rim_recv)

    active = [active_ref[:, lanes(t)] * wet_ref[:, lanes(t)] for t in range(tiles)]
    inputs = (east_ref, north_ref, salt_ref)

    def mask_chunk(c):
        for kk in range(CHUNK):
            k = c * CHUNK + kk
            for t in range(tiles):
                live = active[t] > k
                for f in range(3):
                    q0[f, k, :, lanes(t)] = jnp.where(live, inputs[f][k, :, lanes(t)], 0.0)

    def first(c, carry):
        mask_chunk(c)
        pack(q0, 0, c)
        return carry

    lax.fori_loop(0, chunks, first, 0)

    stat_parts = (
        [surface_ref[:, lanes(t)] for t in range(tiles)],
        [wet_ref[:, lanes(t)].astype(jnp.float32) for t in range(tiles)],
    )
    for f in range(2):
        for t in range(tiles):
            stat_c[f, :, lanes(t)] = stat_parts[f][t]
            all_stat[own, f, :, lanes(t)] = stat_parts[f][t]
        stat_e[f] = jnp.where(lane < LANES // 2, stat_parts[f][0], stat_parts[f][-1])

    pl.semaphore_wait(barrier, count)

    def first_launch(c, carry):
        launch(0, c)
        return carry

    lax.fori_loop(0, chunks, first_launch, 0)
    far(lambda o, side: far_copy(stat_kind, o, side).start())

    def slope8(a, b, c, d):
        return 8.0 * (a - b) - (c - d)

    def run_stage(stage, src, dst, weight0, weight1):
        def body(c, carry):
            press_e, press_n, sum_e, sum_n = [list(x) for x in carry]
            arrive(stage, c)
            rims = jnp.where(lane % 4 < 2, recv_y[stage, 0, c], recv_y[stage, 1, c])
            for kk in range(CHUNK):
                k = c * CHUNK + kk
                fields = []
                for f in range(3):
                    position = f * CHUNK + kk
                    group, m = position // 4, position % 4
                    rim = pltpu.roll(rims, (-(4 * position + 2)) % LANES, 1)
                    parts = [src[f, k, :, lanes(t)] for t in range(tiles)]
                    per_tile = []
                    for t in range(tiles):
                        q = parts[t]
                        after = parts[t + 1] if t + 1 < tiles else rim
                        before = parts[t - 1] if t > 0 else rim
                        ends = jnp.where(
                            pair == m,
                            recv_x[stage, 0, c, group, :, lanes(t)],
                            recv_x[stage, 1, c, group, :, lanes(t)],
                        )
                        if m != 3:
                            ends = pltpu.roll(ends, (-(2 * m + 2)) % ROWS, 0)
                        e1 = pltpu.roll(jnp.where(row < 1, ends, q), ROWS - 1, 0)
                        e2 = pltpu.roll(jnp.where(row < 2, ends, q), ROWS - 2, 0)
                        w1 = pltpu.roll(jnp.where(row >= ROWS - 1, ends, q), 1, 0)
                        w2 = pltpu.roll(jnp.where(row >= ROWS - 2, ends, q), 2, 0)
                        n1 = pltpu.roll(jnp.where(lane < 1, after, q), LANES - 1, 1)
                        n2 = pltpu.roll(jnp.where(lane < 2, after, q), LANES - 2, 1)
                        s1 = pltpu.roll(jnp.where(lane >= LANES - 1, before, q), 1, 1)
                        s2 = pltpu.roll(jnp.where(lane >= LANES - 2, before, q), 2, 1)
                        dx = slope8(e1, w1, e2, w2)
                        dy = slope8(n1, s1, n2, s2)
                        lap = ((e1 + w1) + (n1 + s1)) - 4.0 * q
                        per_tile.append((q, dx, dy, lap))
                    fields.append(per_tile)
                for t in range(tiles):
                    live = active[t] > k
                    (u, ux, uy, ul), (v, vx, vy, vl), (s, sx, sy, sl) = [
                        fields[f][t] for f in range(3)
                    ]
                    press_e[t] = press_e[t] + sx
                    press_n[t] = press_n[t] + sy
                    um = u * (-1.0 / 12.0)
                    vm = v * (-1.0 / 12.0)
                    coef = -PRESS_COEF / 12.0
                    ru = (um * ux + vm * uy) + CORIOLIS * v + coef * press_e[t] + VISCOSITY * ul
                    rv = (um * vx + vm * vy) - CORIOLIS * u + coef * press_n[t] + VISCOSITY * vl
                    rs = (um * sx + vm * sy) + DIFFUSIVITY * sl
                    news = []
                    for f, (q, rate) in enumerate(((u, ru), (v, rv), (s, rs))):
                        new = q + TIME_STEP * rate
                        if weight0 is not None:
                            new = weight0 * q0[f, k, :, lanes(t)] + weight1 * new
                        new = jnp.where(live, new, 0.0)
                        news.append(new)
                        if stage == 2 and f == 2:
                            salt_out[k, :, lanes(t)] = new
                        else:
                            dst[f, k, :, lanes(t)] = new
                    if stage == 2:
                        sum_e[t] = sum_e[t] + news[0]
                        sum_n[t] = sum_n[t] + news[1]
            if stage < 2:
                pack(dst, stage + 1, c)
                launch(stage + 1, c)
            return (tuple(press_e), tuple(press_n), tuple(sum_e), tuple(sum_n))

        zeros = (zero,) * tiles
        return lax.fori_loop(0, chunks, body, (zeros, zeros, zeros, zeros))

    run_stage(0, q0, qa, None, None)
    run_stage(1, qa, qb, 0.75, 0.25)
    carry = run_stage(2, qb, qa, 1.0 / 3.0, 2.0 / 3.0)

    for f in range(2):
        flows = [depth_ref[:, lanes(t)] * (carry[2 + f][t] / levels) for t in range(tiles)]
        for t in range(tiles):
            flow_c[f, :, lanes(t)] = flows[t]
            all_flow[own, f, :, lanes(t)] = flows[t]
        flow_e[f] = jnp.where(lane < LANES // 2, flows[0], flows[-1])
    far(lambda o, side: far_copy(flow_kind, o, side).start())
    far(lambda o, side: far_wait(stat_kind, o, side))

    wide = tiles + 1

    def window(everything, edge, f):
        out = []
        for p in range(slots):
            line = [everything[p, f, :, lanes(t)] for t in range(tiles)]
            line.append(jnp.where(lane < LANES // 2, edge[1, p, f], edge[0, p, f]))
            out.append(line)
        return out

    def up(z, p, t):
        after = z[p + 1][t] if p + 1 < slots else zero
        return pltpu.roll(jnp.where(row < 1, after, z[p][t]), ROWS - 1, 0)

    def down(z, p, t):
        before = z[p - 1][t] if p > 0 else zero
        return pltpu.roll(jnp.where(row >= ROWS - 1, before, z[p][t]), 1, 0)

    def right(z, p, t):
        return pltpu.roll(jnp.where(lane < 1, z[p][(t + 1) % wide], z[p][t]), LANES - 1, 1)

    def left(z, p, t):
        return pltpu.roll(jnp.where(lane >= LANES - 1, z[p][(t - 1) % wide], z[p][t]), 1, 1)

    cells = [(p, t) for p in range(slots) for t in range(wide)]

    def grid(make):
        return [[make(p, t) for t in range(wide)] for p in range(slots)]

    x = window(all_stat, rim_stat, 0)
    wet = window(all_stat, rim_stat, 1)
    wet6 = grid(lambda p, t: wet[p][t] * (1.0 / 6.0))
    diag = grid(lambda p, t: wet[p][t] * SIGMA_SHIFT + (1.0 - wet[p][t]))

    def apply(e):
        w = grid(lambda p, t: wet[p][t] * e[p][t])
        a = grid(lambda p, t: up(w, p, t) + down(w, p, t))
        b = grid(lambda p, t: 4.0 * w[p][t] + a[p][t])
        return grid(
            lambda p, t: wet6[p][t]
            * ((20.0 * w[p][t] - 4.0 * a[p][t]) - (right(b, p, t) + left(b, p, t)))
            + diag[p][t] * e[p][t]
        )

    image = apply(x)

    far(lambda o, side: far_wait(flow_kind, o, side))
    fe = window(all_flow, rim_flow, 0)
    fn = window(all_flow, rim_flow, 1)

    def right_side(p, t):
        div = (up(fe, p, t) - down(fe, p, t)) * 0.5 + (right(fn, p, t) - left(fn, p, t)) * 0.5
        return wet[p][t] * (SIGMA_SHIFT * x[p][t] - DIVERGENCE_COEF * div)

    rhs = grid(right_side)
    r = grid(lambda p, t: rhs[p][t] - image[p][t])
    d = grid(lambda p, t: r[p][t] * (1.0 / CHEB_CENTER))
    keeps, gains = cheb_table(ITERS)
    for index in range(ITERS):
        x = grid(lambda p, t: x[p][t] + d[p][t])
        if index < ITERS - 1:
            image = apply(d)
            r = grid(lambda p, t: r[p][t] - image[p][t])
            d = grid(lambda p, t: keeps[index] * d[p][t] + gains[index] * r[p][t])

    for t in range(wide):
        xs[0, t] = zero
        xs[slots + 1, t] = zero
    for p, t in cells:
        xs[p + 1, t] = x[p][t]
    mine = [[xs[own + i, t] for t in range(wide)] for i in range(3)]
    slope_e = []
    slope_n = []
    for t in range(tiles):
        surface_out[:, lanes(t)] = mine[1][t]
        above = pltpu.roll(jnp.where(row < 1, mine[2][t], mine[1][t]), ROWS - 1, 0)
        below = pltpu.roll(jnp.where(row >= ROWS - 1, mine[0][t], mine[1][t]), 1, 0)
        slope_e.append((above - below) * 0.5)
        slope_n.append((right(mine, 1, t) - left(mine, 1, t)) * 0.5)

    def last(c, carry):
        for kk in range(CHUNK):
            k = c * CHUNK + kk
            for t in range(tiles):
                live = active[t] > k
                east_out[k, :, lanes(t)] = jnp.where(live, qa[0, k, :, lanes(t)] - slope_e[t], 0.0)
                north_out[k, :, lanes(t)] = jnp.where(live, qa[1, k, :, lanes(t)] - slope_n[t], 0.0)
        for stage in range(3):
            drain(stage, c)
        return carry

    lax.fori_loop(0, chunks, last, 0)
    far(lambda o, side: far_copy(stat_kind, o, side).wait_send())
    far(lambda o, side: far_copy(flow_kind, o, side).wait_send())


def solution(mesh):
    nx, ny = mesh.shape["gx"], mesh.shape["gy"]

    def local(east, north, salt, surface, depth, wet, active):
        levels, rows, width = east.shape
        assert rows == ROWS and width % LANES == 0 and levels % CHUNK == 0
        tiles = width // LANES
        chunks = levels // CHUNK
        groups = 3 * CHUNK // 4
        reach = min(nx - 1, -(-(ITERS + 2) // ROWS))
        slots = min(nx, 2 * reach + 1)
        f32 = jnp.float32
        vmem = pltpu.VMEM
        dma = pltpu.SemaphoreType.DMA
        block = pl.BlockSpec(memory_space=pltpu.VMEM)
        state = jax.ShapeDtypeStruct(east.shape, f32)
        span = 2 * reach + 1
        return pl.pallas_call(
            functools.partial(kernel, nx, ny, reach, slots),
            out_shape=(state, state, state, jax.ShapeDtypeStruct(surface.shape, f32)),
            in_specs=[block] * 7,
            out_specs=(block,) * 4,
            scratch_shapes=[
                vmem((3, levels, rows, width), f32),
                vmem((3, levels, rows, width), f32),
                vmem((3, levels, rows, width), f32),
                vmem((3, 2, chunks, groups, rows, width), f32),
                vmem((3, 2, chunks, groups, rows, width), f32),
                vmem((3, chunks, rows, LANES), f32),
                vmem((3, 2, chunks, rows, LANES), f32),
                vmem((2, rows, width), f32),
                vmem((2, rows, LANES), f32),
                vmem((2, rows, width), f32),
                vmem((2, rows, LANES), f32),
                vmem((slots, 2, rows, width), f32),
                vmem((2, slots, 2, rows, LANES), f32),
                vmem((slots, 2, rows, width), f32),
                vmem((2, slots, 2, rows, LANES), f32),
                vmem((slots + 2, tiles + 1, rows, LANES), f32),
                dma((3, 2, chunks)),
                dma((3, 2, chunks)),
                dma((3, 2, chunks)),
                dma((3, 2, chunks)),
                dma((span,)),
                dma((slots,)),
                dma((2, span)),
                dma((2, slots)),
                dma((span,)),
                dma((slots,)),
                dma((2, span)),
                dma((2, slots)),
            ],
            compiler_params=pltpu.CompilerParams(
                collective_id=0, has_side_effects=True, vmem_limit_bytes=48 * 1024 * 1024
            ),
        )(east, north, salt, surface, depth, wet, active)

    return jax.shard_map(
        local,
        mesh=mesh,
        in_specs=(
            P(None, "gx", "gy"),
            P(None, "gx", "gy"),
            P(None, "gx", "gy"),
            P("gx", "gy"),
            P("gx", "gy"),
            P("gx", "gy"),
            P("gx", "gy"),
        ),
        out_specs=(P(None, "gx", "gy"), P(None, "gx", "gy"), P(None, "gx", "gy"), P("gx", "gy")),
        check_vma=False,
    )
```

time: 245 us -> 37.8 us (0.15)
  the two profiles are of different devices: /device:TPU:22 before, /device:TPU:0 now
where the time goes in v1:
time: 37.8 us; the launch traced here: 37.4 us
  Pallas kernels  28.1 us (74%)
  local copies, waits for them, and re-layouts  8.6 us (23%)
  between operations  0.66 us (2%)
    pallas_call x1, Pallas kernels, local(): pl.pallas_call(functools.partial(kernel, nx, ny, reach, slots), out_shape...  28.1 us
    unnamed x18, local copies, waits for them, and re-layouts  8.6 us

profile of v1, /device:TPU:0, one launch (start us, length us, event | category | flops | bytes accessed | tf_op | source)
XLA Modules:
  0.0 37.4 jit_solution(6897906980310871507)
XLA Ops:
  0.6 0.0 copy-start
  0.6 1.0 %copy-done = f32[48,8,256]{2,1,0:T(8,128)S(1)} copy-done((f32[48,8,256]{2,1,0:T(8,128)S(1)}, f32[48,8,256]{2,1,0:T(8,128)}, u32[]{:S(2)}) %copy-start) | copy-done | bytes 393240
  1.6 0.0 copy-start.1
  1.6 1.0 %copy-done.1 = f32[48,8,256]{2,1,0:T(8,128)S(1)} copy-done((f32[48,8,256]{2,1,0:T(8,128)S(1)}, f32[48,8,256]{2,1,0:T(8,128)}, u32[]{:S(2)}) %copy-start.1) | copy-done | bytes 393240
  2.6 0.0 copy-start.2
  2.6 1.0 %copy-done.2 = f32[48,8,256]{2,1,0:T(8,128)S(1)} copy-done((f32[48,8,256]{2,1,0:T(8,128)S(1)}, f32[48,8,256]{2,1,0:T(8,128)}, u32[]{:S(2)}) %copy-start.2) | copy-done | bytes 393240
  3.6 0.0 copy-start.3
  3.6 0.7 %copy-done.3 = f32[8,256]{1,0:T(8,128)S(1)} copy-done((f32[8,256]{1,0:T(8,128)S(1)}, f32[8,256]{1,0:T(8,128)}, u32[]{:S(2)}) %copy-start.3) | copy-done | bytes 8216
  4.3 0.0 copy-start.4
  4.3 0.7 %copy-done.4 = f32[8,256]{1,0:T(8,128)S(1)} copy-done((f32[8,256]{1,0:T(8,128)S(1)}, f32[8,256]{1,0:T(8,128)}, u32[]{:S(2)}) %copy-start.4) | copy-done | bytes 8216
  5.0 0.0 copy-start.5
  5.0 0.7 %copy-done.5 = s32[8,256]{1,0:T(8,128)S(1)} copy-done((s32[8,256]{1,0:T(8,128)S(1)}, s32[8,256]{1,0:T(8,128)}, u32[]{:S(2)}) %copy-start.5) | copy-done | bytes 8216
  5.7 0.0 copy-start.6
  5.7 0.7 %copy-done.6 = s32[8,256]{1,0:T(8,128)S(1)} copy-done((s32[8,256]{1,0:T(8,128)S(1)}, s32[8,256]{1,0:T(8,128)}, u32[]{:S(2)}) %copy-start.6) | copy-done | bytes 8216
  6.4 28.1 %shard_map.102 = (f32[48,8,256]{2,1,0:T(8,128)S(1)}, f32[48,8,256]{2,1,0:T(8,128)S(1)}, f32[48,8,256]{2,1,0:T(8,128)S(1)}, f32[8,256]{1,0:T(8,128)S(1)}) custom-call(f32[48,8,256]{2,1,0:T(8,128)S(1)} %copy-done, f32[48,8,256]{2,1,0:T(8,128)S(1)} %copy-done.1, f32[48,8,256]{2,1,0:T(8,128)S(1)} %copy-done.2, f32[8,256]{1,0:T(8,128)S(1)} %copy-done.3, ...), custom_call_target="tpu_custom_call" | custom-call | tf_op jit(solution)/shard_map/pallas_call | solution.py:474
  34.5 0.7 %copy.15 = f32[48,8,256]{2,1,0:T(8,128)} copy(f32[48,8,256]{2,1,0:T(8,128)S(1)} %get-tuple-element.8) | data formatting | bytes 786432
  35.3 0.7 %copy.16 = f32[48,8,256]{2,1,0:T(8,128)} copy(f32[48,8,256]{2,1,0:T(8,128)S(1)} %get-tuple-element.9) | data formatting | bytes 786432
  36.0 0.7 %copy.17 = f32[48,8,256]{2,1,0:T(8,128)} copy(f32[48,8,256]{2,1,0:T(8,128)S(1)} %get-tuple-element.10) | data formatting | bytes 786432
  36.8 0.6 %copy.18 = f32[8,256]{1,0:T(8,128)} copy(f32[8,256]{1,0:T(8,128)S(1)} %get-tuple-element.11) | data formatting | bytes 16384
Async XLA Ops:
  0.6 1.0 %copy-start = (f32[48,8,256]{2,1,0:T(8,128)S(1)}, f32[48,8,256]{2,1,0:T(8,128)}, u32[]{:S(2)}) copy-start(f32[48,8,256]{2,1,0:T(8,128)} %east_ref.1) | copy-start | bytes 1179652
  1.6 1.0 %copy-start.1 = (f32[48,8,256]{2,1,0:T(8,128)S(1)}, f32[48,8,256]{2,1,0:T(8,128)}, u32[]{:S(2)}) copy-start(f32[48,8,256]{2,1,0:T(8,128)} %north_ref.1) | copy-start | bytes 1179652
  2.6 1.0 %copy-start.2 = (f32[48,8,256]{2,1,0:T(8,128)S(1)}, f32[48,8,256]{2,1,0:T(8,128)}, u32[]{:S(2)}) copy-start(f32[48,8,256]{2,1,0:T(8,128)} %salt_ref.1) | copy-start | bytes 1179652
  3.6 0.7 %copy-start.3 = (f32[8,256]{1,0:T(8,128)S(1)}, f32[8,256]{1,0:T(8,128)}, u32[]{:S(2)}) copy-start(f32[8,256]{1,0:T(8,128)} %surface_ref.1) | copy-start | bytes 24580
  4.3 0.7 %copy-start.4 = (f32[8,256]{1,0:T(8,128)S(1)}, f32[8,256]{1,0:T(8,128)}, u32[]{:S(2)}) copy-start(f32[8,256]{1,0:T(8,128)} %depth_ref.1) | copy-start | bytes 24580
  5.0 0.7 %copy-start.5 = (s32[8,256]{1,0:T(8,128)S(1)}, s32[8,256]{1,0:T(8,128)}, u32[]{:S(2)}) copy-start(s32[8,256]{1,0:T(8,128)} %wet_ref.1) | copy-start | bytes 24580
  5.7 0.7 %copy-start.6 = (s32[8,256]{1,0:T(8,128)S(1)}, s32[8,256]{1,0:T(8,128)}, u32[]{:S(2)}) copy-start(s32[8,256]{1,0:T(8,128)} %active_ref.1) | copy-start | bytes 24580

commit v2 on v1

--- a/solution.py
+++ b/solution.py
@@ -40,8 +40,9 @@
 
 def kernel(
     nx, ny, reach, slots,
-    east_ref, north_ref, salt_ref, surface_ref, depth_ref, wet_ref, active_ref,
-    east_out, north_out, salt_out, surface_out,
+    east_hbm, north_hbm, salt_hbm, surface_hbm, depth_hbm, wet_hbm, active_hbm,
+    state_out, slope_out, surface_out,
+    east_ref, north_ref, salt_ref, surface_ref, depth_ref, wet_ref, active_ref, load_sem,
     q0, qa, qb, send_x, recv_x, send_y, recv_y,
     stat_c, stat_e, flow_c, flow_e, all_stat, rim_stat, all_flow, rim_flow, xs,
     x_send, x_recv, y_send, y_recv,
@@ -71,6 +72,17 @@
         return jnp.logical_and(
             jnp.logical_and(x >= 0, x < nx), jnp.logical_and(y >= 0, y < ny)
         )
+
+    loads = [
+        pltpu.make_async_copy(source, target, load_sem.at[i])
+        for i, (source, target) in enumerate((
+            (active_hbm, active_ref), (wet_hbm, wet_ref), (east_hbm, east_ref),
+            (north_hbm, north_ref), (salt_hbm, salt_ref), (surface_hbm, surface_ref),
+            (depth_hbm, depth_ref),
+        ))
+    ]
+    for load in loads:
+        load.start()
 
     offsets = [o for o in range(-reach, reach + 1)]
     partners = [(o, side) for o in offsets for side in (-1, 0, 1) if (o, side) != (0, 0)]
@@ -231,6 +243,9 @@
                  stat_send, stat_recv, stat_rim_send, stat_rim_recv)
     flow_kind = (flow_c, flow_e, all_flow, rim_flow,
                  flow_send, flow_recv, flow_rim_send, flow_rim_recv)
+
+    for load in loads:
+        load.wait()
 
     active = [active_ref[:, lanes(t)] * wet_ref[:, lanes(t)] for t in range(tiles)]
     inputs = (east_ref, north_ref, salt_ref)
@@ -330,10 +345,7 @@
                             new = weight0 * q0[f, k, :, lanes(t)] + weight1 * new
                         new = jnp.where(live, new, 0.0)
                         news.append(new)
-                        if stage == 2 and f == 2:
-                            salt_out[k, :, lanes(t)] = new
-                        else:
-                            dst[f, k, :, lanes(t)] = new
+                        dst[f, k, :, lanes(t)] = new
                     if stage == 2:
                         sum_e[t] = sum_e[t] + news[0]
                         sum_n[t] = sum_n[t] + news[1]
@@ -347,7 +359,7 @@
 
     run_stage(0, q0, qa, None, None)
     run_stage(1, qa, qb, 0.75, 0.25)
-    carry = run_stage(2, qb, qa, 1.0 / 3.0, 2.0 / 3.0)
+    carry = run_stage(2, qb, state_out, 1.0 / 3.0, 2.0 / 3.0)
 
     for f in range(2):
         flows = [depth_ref[:, lanes(t)] * (carry[2 + f][t] / levels) for t in range(tiles)]
@@ -429,22 +441,14 @@
     for p, t in cells:
         xs[p + 1, t] = x[p][t]
     mine = [[xs[own + i, t] for t in range(wide)] for i in range(3)]
-    slope_e = []
-    slope_n = []
     for t in range(tiles):
         surface_out[:, lanes(t)] = mine[1][t]
         above = pltpu.roll(jnp.where(row < 1, mine[2][t], mine[1][t]), ROWS - 1, 0)
         below = pltpu.roll(jnp.where(row >= ROWS - 1, mine[0][t], mine[1][t]), 1, 0)
-        slope_e.append((above - below) * 0.5)
-        slope_n.append((right(mine, 1, t) - left(mine, 1, t)) * 0.5)
+        slope_out[0, :, lanes(t)] = (above - below) * 0.5
+        slope_out[1, :, lanes(t)] = (right(mine, 1, t) - left(mine, 1, t)) * 0.5
 
     def last(c, carry):
-        for kk in range(CHUNK):
-            k = c * CHUNK + kk
-            for t in range(tiles):
-                live = active[t] > k
-                east_out[k, :, lanes(t)] = jnp.where(live, qa[0, k, :, lanes(t)] - slope_e[t], 0.0)
-                north_out[k, :, lanes(t)] = jnp.where(live, qa[1, k, :, lanes(t)] - slope_n[t], 0.0)
         for stage in range(3):
             drain(stage, c)
         return carry
@@ -452,6 +456,29 @@
     lax.fori_loop(0, chunks, last, 0)
     far(lambda o, side: far_copy(stat_kind, o, side).wait_send())
     far(lambda o, side: far_copy(flow_kind, o, side).wait_send())
+
+
+def finish(
+    state_ref, slope_ref, surface_ref, wet_ref, active_ref,
+    east_out, north_out, salt_out, surface_out, held, sems,
+):
+    early = (
+        pltpu.make_async_copy(state_ref.at[2], salt_out, sems.at[0]),
+        pltpu.make_async_copy(surface_ref, surface_out, sems.at[1]),
+    )
+    for copy in early:
+        copy.start()
+    levels = held.shape[1]
+    active = active_ref[...] * wet_ref[...]
+    slopes = (slope_ref[0], slope_ref[1])
+    for f in range(2):
+        for k in range(levels):
+            held[f, k] = jnp.where(active > k, state_ref[f, k] - slopes[f], 0.0)
+        pltpu.make_async_copy(held.at[f], (east_out, north_out)[f], sems.at[2 + f]).start()
+    for f in range(2):
+        pltpu.make_async_copy(held.at[f], (east_out, north_out)[f], sems.at[2 + f]).wait()
+    for copy in early:
+        copy.wait()
 
 
 def solution(mesh):
@@ -471,12 +498,25 @@
         block = pl.BlockSpec(memory_space=pltpu.VMEM)
         state = jax.ShapeDtypeStruct(east.shape, f32)
         span = 2 * reach + 1
-        return pl.pallas_call(
+        hbm = pl.BlockSpec(memory_space=pltpu.HBM)
+        state3, slopes, surface_next = pl.pallas_call(
             functools.partial(kernel, nx, ny, reach, slots),
-            out_shape=(state, state, state, jax.ShapeDtypeStruct(surface.shape, f32)),
-            in_specs=[block] * 7,
-            out_specs=(block,) * 4,
+            out_shape=(
+                jax.ShapeDtypeStruct((3,) + east.shape, f32),
+                jax.ShapeDtypeStruct((2,) + surface.shape, f32),
+                jax.ShapeDtypeStruct(surface.shape, f32),
+            ),
+            in_specs=[hbm] * 7,
+            out_specs=(block,) * 3,
             scratch_shapes=[
+                vmem(east.shape, f32),
+                vmem(east.shape, f32),
+                vmem(east.shape, f32),
+                vmem(surface.shape, f32),
+                vmem(surface.shape, f32),
+                vmem(surface.shape, jnp.int32),
+                vmem(surface.shape, jnp.int32),
+                dma((7,)),
                 vmem((3, levels, rows, width), f32),
                 vmem((3, levels, rows, width), f32),
                 vmem((3, levels, rows, width), f32),
@@ -509,7 +549,18 @@
             compiler_params=pltpu.CompilerParams(
                 collective_id=0, has_side_effects=True, vmem_limit_bytes=48 * 1024 * 1024
             ),
-        )(east, north, salt, surface, depth, wet, active)
+        )(*[
+            pltpu.with_memory_space_constraint(z, pltpu.HBM)
+            for z in (east, north, salt, surface, depth, wet, active)
+        ])
+        return pl.pallas_call(
+            finish,
+            out_shape=(state, state, state, jax.ShapeDtypeStruct(surface.shape, f32)),
+            in_specs=[block] * 5,
+            out_specs=(hbm,) * 4,
+            scratch_shapes=[vmem((2,) + east.shape, f32), dma((4,))],
+            compiler_params=pltpu.CompilerParams(vmem_limit_bytes=8 * 1024 * 1024),
+        )(state3, slopes, surface_next, wet, active)
 
     return jax.shard_map(
         local,

time: 37.8 us -> 30.1 us (0.80)
  local copies, waits for them, and re-layouts: 8.6 us -> 0.01 us
  Pallas kernels: 28.1 us -> 29.2 us
    unnamed x18 -> x4, local copies, waits for them, and re-layouts: 8.6 us -> 0.01 us
    pallas_call x0 -> x1, Pallas kernels: none -> 1.05 us  [local(): pl.pallas_call(finish, out_shape=(state, state, state, jax.ShapeDtypeStru...]
where the time goes in v2:
time: 30.1 us; the launch traced here: 29.9 us
  Pallas kernels  29.2 us (97%)
  between operations  0.67 us (2%)
    pallas_call x1, Pallas kernels, local(): pl.pallas_call(functools.partial(kernel, nx, ny, reach, slots), out_shape...  28.2 us
    pallas_call x1, Pallas kernels, local(): pl.pallas_call(finish, out_shape=(state, state, state, jax.ShapeDtypeStru...  1.05 us

profile of v2, /device:TPU:0, one launch (start us, length us, event | category | flops | bytes accessed | tf_op | source)
XLA Modules:
  0.0 29.9 jit_solution(10472337690190467314)
XLA Ops:
  0.6 0.0 copy-start.1
  0.6 0.0 copy-start
  0.7 28.2 %shard_map.102 = (f32[3,48,8,256]{3,2,1,0:T(8,128)S(1)}, f32[2,8,256]{2,1,0:T(8,128)S(1)}, f32[8,256]{1,0:T(8,128)S(1)}) custom-call(f32[48,8,256]{2,1,0:T(8,128)} %east_hbm.1, f32[48,8,256]{2,1,0:T(8,128)} %north_hbm.1, f32[48,8,256]{2,1,0:T(8,128)} %salt_hbm.1, f32[8,256]{1,0:T(8,128)} %surface_hbm.1, f32[8,256]{1,0:T(8,128)} %depth_hbm.1, ...), custom_call_target="tpu_custom_call" | custom-call | tf_op jit(solution)/shard_map/pallas_call | solution.py:502
  28.8 0.0 copy-done.1
  28.8 0.0 copy-done
  28.9 1.0 %shard_map.103 = (f32[48,8,256]{2,1,0:T(8,128)}, f32[48,8,256]{2,1,0:T(8,128)}, f32[48,8,256]{2,1,0:T(8,128)}, f32[8,256]{1,0:T(8,128)}) custom-call(f32[3,48,8,256]{3,2,1,0:T(8,128)S(1)} %get-tuple-element.7.state_ref, f32[2,8,256]{2,1,0:T(8,128)S(1)} %get-tuple-element.8.slope_ref, f32[8,256]{1,0:T(8,128)S(1)} %get-tuple-element.9.surface_ref, ...), custom_call_target="tpu_custom_call" | custom-call | tf_op jit(solution)/shard_map/pallas_call | solution.py:556
Async XLA Ops:
  0.6 28.2 %copy-start.1 = (s32[8,256]{1,0:T(8,128)S(1)}, s32[8,256]{1,0:T(8,128)}, u32[]{:S(2)}) copy-start(s32[8,256]{1,0:T(8,128)} %active_ref.1) | copy-start | bytes 24580
  0.6 28.2 %copy-start = (s32[8,256]{1,0:T(8,128)S(1)}, s32[8,256]{1,0:T(8,128)}, u32[]{:S(2)}) copy-start(s32[8,256]{1,0:T(8,128)} %wet_ref.1) | copy-start | bytes 24580

commit v3 on v2

--- a/solution.py
+++ b/solution.py
@@ -43,7 +43,7 @@
     east_hbm, north_hbm, salt_hbm, surface_hbm, depth_hbm, wet_hbm, active_hbm,
     state_out, slope_out, surface_out,
     east_ref, north_ref, salt_ref, surface_ref, depth_ref, wet_ref, active_ref, load_sem,
-    q0, qa, qb, send_x, recv_x, send_y, recv_y,
+    shifts, moved, q0, qa, qb, send_x, recv_x, send_y, recv_y,
     stat_c, stat_e, flow_c, flow_e, all_stat, rim_stat, all_flow, rim_flow, xs,
     x_send, x_recv, y_send, y_recv,
     stat_send, stat_recv, stat_rim_send, stat_rim_recv,
@@ -244,6 +244,27 @@
     flow_kind = (flow_c, flow_e, all_flow, rim_flow,
                  flow_send, flow_recv, flow_rim_send, flow_rim_recv)
 
+    source = lax.broadcasted_iota(jnp.int32, (width, width), 0)
+    target = lax.broadcasted_iota(jnp.int32, (width, width), 1)
+    step = source - target
+    one = jnp.abs(step) == 1
+    sign = jnp.where(step > 0, 1.0, -1.0)
+    slope = jnp.where(one, 8.0 * sign, jnp.where(jnp.abs(step) == 2, -sign, 0.0))
+    shifts[:, :width] = slope.astype(jnp.bfloat16)
+    shifts[:, width:] = jnp.where(one, 1.0, 0.0).astype(jnp.bfloat16)
+
+    def move_chunk(src, c):
+        for f in range(3):
+            whole = src[f, pl.ds(c * CHUNK, CHUNK)].reshape(CHUNK * ROWS, width)
+            high = whole.astype(jnp.bfloat16)
+            rest = whole - high.astype(jnp.float32)
+            middle = rest.astype(jnp.bfloat16)
+            low = (rest - middle.astype(jnp.float32)).astype(jnp.bfloat16)
+            total = jnp.dot(low, shifts[...], preferred_element_type=jnp.float32)
+            total = total + jnp.dot(middle, shifts[...], preferred_element_type=jnp.float32)
+            total = total + jnp.dot(high, shifts[...], preferred_element_type=jnp.float32)
+            moved[f] = total.reshape(CHUNK, ROWS, 2 * width)
+
     for load in loads:
         load.wait()
 
@@ -292,19 +313,28 @@
             press_e, press_n, sum_e, sum_n = [list(x) for x in carry]
             arrive(stage, c)
             rims = jnp.where(lane % 4 < 2, recv_y[stage, 0, c], recv_y[stage, 1, c])
+            move_chunk(src, c)
+            r1, r2 = pltpu.roll(rims, LANES - 1, 1), pltpu.roll(rims, LANES - 2, 1)
+            l1, l2 = pltpu.roll(rims, 1, 1), pltpu.roll(rims, 2, 1)
+            quarter = lane % 4
+            rim_slope = jnp.where(
+                quarter < 2,
+                jnp.where(quarter == 0, -r2, 8.0 * r1 - r2),
+                jnp.where(quarter == 2, l2 - 8.0 * l1, l2),
+            )
+            rim_sum = jnp.where(quarter == 1, r1, jnp.where(quarter == 2, l1, 0.0))
             for kk in range(CHUNK):
                 k = c * CHUNK + kk
                 fields = []
                 for f in range(3):
                     position = f * CHUNK + kk
                     group, m = position // 4, position % 4
-                    rim = pltpu.roll(rims, (-(4 * position + 2)) % LANES, 1)
+                    extra_slope = pltpu.roll(rim_slope, (-(4 * position + 2)) % LANES, 1)
+                    extra_sum = pltpu.roll(rim_sum, (-(4 * position + 2)) % LANES, 1)
                     parts = [src[f, k, :, lanes(t)] for t in range(tiles)]
                     per_tile = []
                     for t in range(tiles):
                         q = parts[t]
-                        after = parts[t + 1] if t + 1 < tiles else rim
-                        before = parts[t - 1] if t > 0 else rim
                         ends = jnp.where(
                             pair == m,
                             recv_x[stage, 0, c, group, :, lanes(t)],
@@ -316,13 +346,16 @@
                         e2 = pltpu.roll(jnp.where(row < 2, ends, q), ROWS - 2, 0)
                         w1 = pltpu.roll(jnp.where(row >= ROWS - 1, ends, q), 1, 0)
                         w2 = pltpu.roll(jnp.where(row >= ROWS - 2, ends, q), 2, 0)
-                        n1 = pltpu.roll(jnp.where(lane < 1, after, q), LANES - 1, 1)
-                        n2 = pltpu.roll(jnp.where(lane < 2, after, q), LANES - 2, 1)
-                        s1 = pltpu.roll(jnp.where(lane >= LANES - 1, before, q), 1, 1)
-                        s2 = pltpu.roll(jnp.where(lane >= LANES - 2, before, q), 2, 1)
+                        dy = moved[f, kk, :, lanes(t)]
+                        sides = moved[f, kk, :, lanes(tiles + t)]
+                        if t == 0:
+                            dy = dy + jnp.where(lane < 2, extra_slope, 0.0)
+                            sides = sides + jnp.where(lane < 2, extra_sum, 0.0)
+                        if t == tiles - 1:
+                            dy = dy + jnp.where(lane >= LANES - 2, extra_slope, 0.0)
+                            sides = sides + jnp.where(lane >= LANES - 2, extra_sum, 0.0)
                         dx = slope8(e1, w1, e2, w2)
-                        dy = slope8(n1, s1, n2, s2)
-                        lap = ((e1 + w1) + (n1 + s1)) - 4.0 * q
+                        lap = ((e1 + w1) + sides) - 4.0 * q
                         per_tile.append((q, dx, dy, lap))
                     fields.append(per_tile)
                 for t in range(tiles):
@@ -517,6 +550,8 @@
                 vmem(surface.shape, jnp.int32),
                 vmem(surface.shape, jnp.int32),
                 dma((7,)),
+                vmem((width, 2 * width), jnp.bfloat16),
+                vmem((3, CHUNK, rows, 2 * width), f32),
                 vmem((3, levels, rows, width), f32),
                 vmem((3, levels, rows, width), f32),
                 vmem((3, levels, rows, width), f32),

time: 30.1 us -> 29.6 us (0.983)
  Pallas kernels: 29.2 us -> 28.8 us
    pallas_call x1, Pallas kernels: 28.2 us -> 27.8 us  [local(): pl.pallas_call(functools.partial(kernel, nx, ny, reach, slots), out_shape...]
where the time goes in v3:
time: 29.6 us; the launch traced here: 29.5 us
  Pallas kernels  28.8 us (97%)
  between operations  0.67 us (2%)
    pallas_call x1, Pallas kernels, local(): pl.pallas_call(functools.partial(kernel, nx, ny, reach, slots), out_shape...  27.8 us
    pallas_call x1, Pallas kernels, local(): pl.pallas_call(finish, out_shape=(state, state, state, jax.ShapeDtypeStru...  1.05 us

profile of v3, /device:TPU:0, one launch (start us, length us, event | category | flops | bytes accessed | tf_op | source)
XLA Modules:
  0.0 29.5 jit_solution(4481031671880758810)
XLA Ops:
  0.6 0.0 copy-start.1
  0.6 0.0 copy-start
  0.7 27.8 %shard_map.102 = (f32[3,48,8,256]{3,2,1,0:T(8,128)S(1)}, f32[2,8,256]{2,1,0:T(8,128)S(1)}, f32[8,256]{1,0:T(8,128)S(1)}) custom-call(f32[48,8,256]{2,1,0:T(8,128)} %east_hbm.1, f32[48,8,256]{2,1,0:T(8,128)} %north_hbm.1, f32[48,8,256]{2,1,0:T(8,128)} %salt_hbm.1, f32[8,256]{1,0:T(8,128)} %surface_hbm.1, f32[8,256]{1,0:T(8,128)} %depth_hbm.1, ...), custom_call_target="tpu_custom_call" | custom-call | tf_op jit(solution)/shard_map/pallas_call | solution.py:535
  28.4 0.0 copy-done.1
  28.4 0.0 copy-done
  28.4 1.0 %shard_map.103 = (f32[48,8,256]{2,1,0:T(8,128)}, f32[48,8,256]{2,1,0:T(8,128)}, f32[48,8,256]{2,1,0:T(8,128)}, f32[8,256]{1,0:T(8,128)}) custom-call(f32[3,48,8,256]{3,2,1,0:T(8,128)S(1)} %get-tuple-element.7.state_ref, f32[2,8,256]{2,1,0:T(8,128)S(1)} %get-tuple-element.8.slope_ref, f32[8,256]{1,0:T(8,128)S(1)} %get-tuple-element.9.surface_ref, ...), custom_call_target="tpu_custom_call" | custom-call | tf_op jit(solution)/shard_map/pallas_call | solution.py:591
Async XLA Ops:
  0.6 27.8 %copy-start.1 = (s32[8,256]{1,0:T(8,128)S(1)}, s32[8,256]{1,0:T(8,128)}, u32[]{:S(2)}) copy-start(s32[8,256]{1,0:T(8,128)} %active_ref.1) | copy-start | bytes 24580
  0.6 27.8 %copy-start = (s32[8,256]{1,0:T(8,128)S(1)}, s32[8,256]{1,0:T(8,128)}, u32[]{:S(2)}) copy-start(s32[8,256]{1,0:T(8,128)} %wet_ref.1) | copy-start | bytes 24580
